TPU v7x, 16 devices: a whole 2x2x2 slice. The times are simulated.
16 devices in a mesh: dp: 2 (over z), ep: 8 (over y, x, core).
Axes of the slice: x: 2, y: 2, z: 2, core: 2. Of those that a mesh axis runs over, the one named last changes fastest.
Arguments:
- x_tokens: bfloat16 [131072, 768], P(('dp', 'ep'))
- expert_id: int32 [131072], P(('dp', 'ep'))
- token_slot: int32 [131072], P(('dp', 'ep'))
- grad_y: bfloat16 [131072, 768], P(('dp', 'ep'))
- w_router: float32 [768, 32], replicated
- w_in: bfloat16 [32, 768, 3072], P('ep')
- w_out: bfloat16 [32, 3072, 768], P('ep')
- row_in: float32 [32, 768], P('ep')
- col_in: float32 [32, 3072], P('ep')
- row_out: float32 [32, 3072], P('ep')
- col_out: float32 [32, 768], P('ep')
- row_router: float32 [768], replicated
- col_router: float32 [32], replicated
Outputs:
- output 1: bfloat16 [32, 768, 3072], P('ep')
- output 2: bfloat16 [32, 3072, 768], P('ep')
- output 3: float32 [768, 32], replicated
- output 4: float32 [32, 768], P('ep')
- output 5: float32 [32, 3072], P('ep')
- output 6: float32 [32, 3072], P('ep')
- output 7: float32 [32, 768], P('ep')
- output 8: float32 [768], replicated
- output 9: float32 [32], replicated
- output 10: bfloat16 [131072, 768], P(('dp', 'ep'))
All inputs are finite; a program needn't handle non-finite values.
Results may differ from a plain program's by a relative error of at most 0.00322.
Values are sent between devices in bfloat16 or wider.
A program may use at most 1 GiB of HBM per device.

v0:
```python
import jax
import jax.numpy as jnp
from jax import lax
from jax.sharding import PartitionSpec as P
import math

OPT_STEP = 2
DECAY_RATE = 1.0 - OPT_STEP ** -0.8
LR_BASE = min(0.01, 1.0 / math.sqrt(OPT_STEP))
AUX_COEF = 0.01
PRECISE = lax.Precision.HIGHEST


def optimizer_step(weight, gradient, row_stat, col_stat):
    grad_sq = gradient * gradient + 1e-30
    row_new = DECAY_RATE * row_stat + (1.0 - DECAY_RATE) * jnp.mean(grad_sq, axis=-1)
    col_new = DECAY_RATE * col_stat + (1.0 - DECAY_RATE) * jnp.mean(grad_sq, axis=-2)
    row_norm = row_new / jnp.mean(row_new, axis=-1, keepdims=True)
    update = gradient * lax.rsqrt(row_norm)[..., :, None] * lax.rsqrt(col_new)[..., None, :]
    upd_rms = jnp.sqrt(jnp.mean(update * update, axis=(-2, -1), keepdims=True))
    update = update / jnp.maximum(1.0, upd_rms)
    w_full = weight.astype(jnp.float32)
    w_rms = jnp.sqrt(jnp.mean(w_full * w_full, axis=(-2, -1), keepdims=True))
    new_weight = w_full - LR_BASE * jnp.maximum(1e-3, w_rms) * update
    return new_weight, row_new, col_new


def solution(mesh):
    ep_size = mesh.shape['ep']
    tok_spec = P(('dp', 'ep'))
    row_spec = P(('dp', 'ep'), None)
    exp_spec = P('ep')
    full_spec = P()

    def local_step(x_tokens, expert_id, token_slot, grad_y, w_router, w_in, w_out, row_in, col_in, row_out, col_out, row_router, col_router):
        tokens, width = x_tokens.shape
        experts_local = w_in.shape[0]
        experts = w_router.shape[1]
        capacity = 5 * tokens // (4 * experts)
        x_wide = x_tokens.astype(jnp.float32)
        logits = jnp.dot(x_wide, w_router, precision=PRECISE)
        gate_probs = jax.nn.softmax(logits, axis=-1)
        onehot = (expert_id[:, None] == jnp.arange(experts)[None, :]).astype(jnp.float32)
        gate_val = jnp.sum(gate_probs * onehot, axis=-1)
        flat_pos = jnp.where(token_slot >= 0, expert_id * capacity + token_slot, experts * capacity)
        src_tok = jnp.full((experts * capacity,), tokens, jnp.int32).at[flat_pos].set(jnp.arange(tokens, dtype=jnp.int32), mode='drop')

        def to_experts(token_rows):
            send_buf = jnp.take(token_rows, src_tok, axis=0, mode='fill', fill_value=0)
            send_buf = send_buf.reshape(ep_size, experts_local, capacity, width)
            recv_buf = lax.all_to_all(send_buf, 'ep', 0, 2, tiled=True)
            return recv_buf.reshape(experts_local, ep_size * capacity, width)

        def to_tokens(expert_rows):
            back_buf = lax.all_to_all(expert_rows.reshape(1, experts_local, ep_size * capacity, width), 'ep', 2, 0, tiled=True)
            back_buf = back_buf.reshape(experts * capacity, width)
            return jnp.take(back_buf, flat_pos, axis=0, mode='fill', fill_value=0)

        recv_x = to_experts(x_tokens)
        pre_act = jnp.einsum('erd,edf->erf', recv_x, w_in, preferred_element_type=jnp.float32).astype(jnp.bfloat16)
        hid_act = jnp.maximum(pre_act, 0)
        exp_out = jnp.einsum('erf,efd->erd', hid_act, w_out, preferred_element_type=jnp.float32).astype(jnp.bfloat16)
        out_tok = to_tokens(exp_out)
        grad_gate = jnp.einsum('td,td->t', grad_y, out_tok, preferred_element_type=jnp.float32)
        grad_h = (gate_val[:, None] * grad_y).astype(jnp.bfloat16)
        recv_gh = to_experts(grad_h)
        grad_act = jnp.einsum('erd,efd->erf', recv_gh, w_out, preferred_element_type=jnp.float32)
        grad_pre = jnp.where(pre_act > 0, grad_act, 0.0).astype(jnp.bfloat16)
        grad_wout = jnp.einsum('erf,erd->efd', hid_act, recv_gh, preferred_element_type=jnp.float32)
        grad_win = jnp.einsum('erd,erf->edf', recv_x, grad_pre, preferred_element_type=jnp.float32)
        grad_buf = jnp.einsum('erf,edf->erd', grad_pre, w_in, preferred_element_type=jnp.float32).astype(jnp.bfloat16)
        dx_expert = to_tokens(grad_buf)
        grad_win = lax.psum(grad_win, 'dp')
        grad_wout = lax.psum(grad_wout, 'dp')
        route_frac = jnp.mean(onehot, axis=0)
        grad_prob = onehot * grad_gate[:, None] + AUX_COEF * experts * route_frac[None, :] / tokens
        grad_logits = gate_probs * (grad_prob - jnp.sum(gate_probs * grad_prob, axis=-1, keepdims=True))
        grad_router = lax.psum(jnp.einsum('td,te->de', x_wide, grad_logits, precision=PRECISE), ('dp', 'ep'))
        grad_x = (dx_expert.astype(jnp.float32) + jnp.einsum('te,de->td', grad_logits, w_router, precision=PRECISE)).astype(jnp.bfloat16)
        new_in, row_in_new, col_in_new = optimizer_step(w_in, grad_win, row_in, col_in)
        new_out, row_out_new, col_out_new = optimizer_step(w_out, grad_wout, row_out, col_out)
        new_router, row_router_new, col_router_new = optimizer_step(w_router, grad_router, row_router, col_router)
        return (new_in.astype(jnp.bfloat16), new_out.astype(jnp.bfloat16), new_router, row_in_new, col_in_new, row_out_new, col_out_new, row_router_new, col_router_new, grad_x)

    in_specs = (row_spec, tok_spec, tok_spec, row_spec, full_spec, exp_spec, exp_spec, exp_spec, exp_spec, exp_spec, exp_spec, full_spec, full_spec)
    out_specs = (exp_spec, exp_spec, full_spec, exp_spec, exp_spec, exp_spec, exp_spec, full_spec, full_spec, row_spec)
    return jax.shard_map(local_step, mesh=mesh, in_specs=in_specs, out_specs=out_specs, check_vma=False)
```

profile of v0, /device:TPU:0, one launch (start us, length us, event | category | flops | bytes accessed | tf_op | source)
XLA Modules:
  0.0 2895.0 jit_solution(7388481224891477603)
XLA Ops:
  8.6 30.5 %scatter_custom_fusion = s32[10240]{0:T(1024)S(1)} fusion(s32[8192]{0:T(1024)S(1)} %get-tuple-element.35, s32[8192]{0:T(1024)S(1)} %iota.7, s32[]{:T(128)} %constant.51.clone.1), kind=kCustom, calls=%fused_computation.78 | custom fusion | bytes 40964 | tf_op jit(solution)/shard_map/scatter | solution.py:46
  39.1 52.2 %gather_fusion = bf16[10240,768]{1,0:T(8,128)(2,1)} fusion(bf16[8192,768]{1,0:T(8,128)(2,1)} %param.17, s32[10240]{0:T(1024)S(1)} %fusion.33), kind=kCustom, calls=%fused_computation.clone | custom fusion | bytes 31498240 | tf_op jit(solution)/shard_map/jit(_take)/gather | solution.py:49
  101.3 178.4 %all_to_all.60 = bf16[8,4,320,768]{3,2,1,0:T(8,128)(2,1)S(1)} all-to-all(bf16[8,4,320,768]{3,2,1,0:T(8,128)(2,1)S(1)} %bitcast.45), channel_id=1, replica_groups=mesh['dp'=2,'ep'=8] {'ep'}, dimensions={0} | all-to-all | bytes 31457280 | tf_op jit(solution)/shard_map/all_to_all | solution.py:51
  286.0 69.1 %fusion.12 = (u8[2560,3072]{1,0:T(8,128)(4,1)}, bf16[4,2560,3072]{2,1,0:T(8,128)(2,1)}) fusion(bf16[4,2560,768]{2,1,0:T(8,128)(2,1)} %bitcast.49, bf16[4,768,3072]{2,1,0:T(8,128)(2,1)} %param.22), kind=kOutput, calls=%fused_computation.31 | convolution fusion | flops 48562176000 | bytes 105381888 | tf_op jit(solution)/shard_map/erd,edf->erf/dot_general | solution.py:60
  355.1 60.0 %convert_bitcast_fusion.1 = bf16[1,4,2560,768]{3,2,1,0:T(8,128)(2,1)} fusion(bf16[4,3072,768]{2,1,0:T(8,128)(2,1)} %param.23, bf16[4,2560,3072]{2,1,0:T(8,128)(2,1)} %get-tuple-element.39), kind=kOutput, calls=%fused_computation.40 | convolution fusion | flops 48357703680 | bytes 97517568 | tf_op jit(solution)/shard_map/erf,efd->erd/dot_general | solution.py:62
  415.0 21.1 copy.33
  456.4 158.4 %all-to-all-done.2 = bf16[1,4,2560,768]{3,1,0,2:T(4,128)(2,1)} async-done(((bf16[1,4,2560,768]{3,1,0,2:T(4,128)(2,1)}), bf16[1,4,2560,768]{3,1,0,2:T(4,128)(2,1)}, u32[]{:S(2)}, u32[]{:S(2)}) %all-to-all-start.2) | async-done | bytes 15728672 | tf_op jit(solution)/shard_map/all_to_all | solution.py:55
  614.8 15.2 copy.34
  630.0 44.5 %gather_fusion.2 = bf16[8192,768]{1,0:T(8,128)(2,1)} fusion(bf16[10240,768]{1,0:T(8,128)(2,1)} %bitcast.43, s32[8192]{0:T(1024)S(1)} %broadcast_clamp_fusion), kind=kCustom, calls=%fused_computation.1.clone | custom fusion | bytes 25198592 | tf_op jit(solution)/shard_map/jit(_take)/gather | solution.py:57
  693.0 52.2 %gather_fusion.1 = bf16[10240,768]{1,0:T(8,128)(2,1)} fusion(bf16[8192,768]{1,0:T(8,128)(2,1)} %fusion.15, s32[10240]{0:T(1024)S(1)} %copy-done.14), kind=kCustom, calls=%fused_computation.2.clone | custom fusion | bytes 31498240 | tf_op jit(solution)/shard_map/jit(_take)/gather | solution.py:49
  776.4 163.1 %all-to-all-done.1 = bf16[8,4,320,768]{3,2,1,0:T(8,128)(2,1)} async-done(((bf16[8,4,320,768]{3,2,1,0:T(8,128)(2,1)}), bf16[8,4,320,768]{3,2,1,0:T(8,128)(2,1)}, u32[]{:S(2)}, u32[]{:S(2)}) %all-to-all-start.1) | async-done | bytes 15728672 | tf_op jit(solution)/shard_map/all_to_all | solution.py:51
  952.7 60.9 %fusion.2 = f32[4,3072,768]{2,1,0:T(8,128)} fusion(bf16[4,2560,768]{2,1,0:T(8,128)(2,1)} %bitcast.51, bf16[4,2560,3072]{2,1,0:T(8,128)(2,1)} %get-tuple-element.39), kind=kOutput, calls=%fused_computation.11 | convolution fusion | flops 48349839360 | bytes 116391936 | tf_op jit(solution)/shard_map/erf,erd->efd/dot_general | solution.py:69
  1013.6 73.1 %select_convert_fusion = bf16[4,2560,3072]{2,1,0:T(8,128)(2,1)} fusion(bf16[4,2560,768]{2,1,0:T(8,128)(2,1)} %bitcast.52, bf16[4,3072,768]{2,1,0:T(8,128)(2,1)} %param.23, u8[2560,3072]{1,0:T(8,128)(4,1)} %get-tuple-element.38), kind=kOutput, calls=%fused_computation.7 | convolution fusion | flops 48507125760 | bytes 105381888 | tf_op jit(solution)/shard_map/erd,efd->erf/dot_general | solution.py:67
  1086.7 60.2 %fusion.49 = f32[4,768,3072]{2,1,0:T(8,128)} fusion(bf16[4,2560,768]{2,1,0:T(8,128)(2,1)} %bitcast.50, bf16[4,2560,3072]{2,1,0:T(8,128)(2,1)} %select_convert_fusion), kind=kOutput, calls=%fused_computation.105 | convolution fusion | flops 48318382080 | bytes 116391936 | tf_op jit(solution)/shard_map/erd,erf->edf/dot_general | solution.py:70
  1147.0 58.5 %convert_bitcast_fusion = bf16[1,4,2560,768]{3,2,1,0:T(8,128)(2,1)} fusion(bf16[4,2560,3072]{2,1,0:T(8,128)(2,1)} %select_convert_fusion, bf16[4,768,3072]{2,1,0:T(8,128)(2,1)} %param.22), kind=kOutput, calls=%fused_computation.39 | convolution fusion | flops 48326246400 | bytes 97517568 | tf_op jit(solution)/shard_map/erf,edf->erd/dot_general | solution.py:71
  1205.5 21.0 copy.35
  1257.7 147.5 %all-to-all-done.3 = bf16[1,4,2560,768]{3,1,0,2:T(4,128)(2,1)} async-done(((bf16[1,4,2560,768]{3,1,0,2:T(4,128)(2,1)}), bf16[1,4,2560,768]{3,1,0,2:T(4,128)(2,1)}, u32[]{:S(2)}, u32[]{:S(2)}) %all-to-all-start.3) | async-done | bytes 15728672 | tf_op jit(solution)/shard_map/all_to_all | solution.py:55
  1420.4 44.6 %gather_fusion.3 = bf16[8192,768]{1,0:T(8,128)(2,1)} fusion(bf16[10240,768]{1,0:T(8,128)(2,1)} %bitcast.42, s32[8192]{0:T(1024)S(1)} %copy-done.18), kind=kCustom, calls=%fused_computation.3.clone | custom fusion | bytes 25198592 | tf_op jit(solution)/shard_map/jit(_take)/gather | solution.py:57
  1465.1 26.1 add_convert_fusion
  1491.2 1289.6 %all-reduce.6.cloned.1.call-done = (f32[4,768,3072]{2,1,0:T(8,128)}, f32[4,3072,768]{2,1,0:T(8,128)}) async-done(((f32[4,768,3072]{2,1,0:T(8,128)}, f32[4,3072,768]{2,1,0:T(8,128)}), (f32[4,768,3072]{2,1,0:T(8,128)}, f32[4,3072,768]{2,1,0:T(8,128)})) %all-reduce.6.cloned.1.call-update) | async-done | bytes 75497488 | tf_op jit(solution)/shard_map/psum | solution.py:73
  2780.8 16.3 fusion.9
  2811.7 15.9 multiply_reduce_fusion.1
  2836.4 25.8 fusion.5
  2862.2 25.7 fusion.7
  (126 shorter events, 168.2 us)
Async XLA Ops:
  39.1 52.3 %copy-start.22 = (pred[10240]{0:T(1024)(128)(4,1)}, pred[10240]{0:T(1024)(128)(4,1)S(1)}, u32[]{:S(2)}) copy-start(pred[10240]{0:T(1024)(128)(4,1)S(1)} %compare_and_fusion) | copy-start | bytes 30724
  39.1 52.3 %copy-start.13 = (s32[10240]{0:T(1024)}, s32[10240]{0:T(1024)S(1)}, u32[]{:S(2)}) copy-start(s32[10240]{0:T(1024)S(1)} %fusion.33) | copy-start | bytes 122884
  436.1 178.7 %all-to-all-start.2 = ((bf16[1,4,2560,768]{3,1,0,2:T(4,128)(2,1)}), bf16[1,4,2560,768]{3,1,0,2:T(4,128)(2,1)}, u32[]{:S(2)}, u32[]{:S(2)}) async-start(bf16[1,4,2560,768]{3,1,0,2:T(4,128)(2,1)} %copy.33), calls=%async_computation.2 | async-start | bytes 31457280 | tf_op jit(solution)/shard_map/all_to_all | solution.py:55
  456.1 309.8 %copy-start.1 = (f32[8192,32]{0,1:T(8,128)}, f32[8192,32]{0,1:T(8,128)S(1)}, u32[]{:S(2)}) copy-start(f32[8192,32]{0,1:T(8,128)S(1)} %get-tuple-element.37) | copy-start | bytes 3145732
  456.1 309.8 %copy-start.5 = (f32[8192]{0:T(1024)}, f32[8192]{0:T(1024)S(1)}, u32[]{:S(2)}) copy-start(f32[8192]{0:T(1024)S(1)} %get-tuple-element.36) | copy-start | bytes 98308
  456.4 309.6 %copy-start.11 = (f32[8192]{0:T(1024)}, f32[8192]{0:T(1024)S(1)}, u32[]{:S(2)}) copy-start(f32[8192]{0:T(1024)S(1)} %fusion.20) | copy-start | bytes 98308
  456.4 309.6 %copy-start.32 = (f32[32]{0:T(128)}, f32[32]{0:T(128)S(1)}, u32[]{:S(2)}) copy-start(f32[32]{0:T(128)S(1)} %broadcast_multiply_fusion) | copy-start | bytes 388
  456.4 218.1 %copy-start.17 = (s32[8192]{0:T(1024)}, s32[8192]{0:T(1024)S(1)}, u32[]{:S(2)}) copy-start(s32[8192]{0:T(1024)S(1)} %broadcast_clamp_fusion) | copy-start | bytes 98308
  685.9 80.1 %copy-start.9 = (f32[8192]{0:T(1024)}, f32[8192]{0:T(1024)S(1)}, u32[]{:S(2)}) copy-start(f32[8192]{0:T(1024)S(1)} %fusion.16) | copy-start | bytes 98308
  686.5 79.5 %copy-start.15 = (f32[8192]{0:T(1024)}, f32[8192]{0:T(1024)S(1)}, u32[]{:S(2)}) copy-start(f32[8192]{0:T(1024)S(1)} %get-tuple-element.16) | copy-start | bytes 98308
  693.0 52.2 %copy-start.23 = (pred[10240]{0:T(1024)(128)(4,1)S(1)}, pred[10240]{0:T(1024)(128)(4,1)}, u32[]{:S(2)}) copy-start(pred[10240]{0:T(1024)(128)(4,1)} %copy-done.22) | copy-start | bytes 30724
  760.3 179.3 %all-to-all-start.1 = ((bf16[8,4,320,768]{3,2,1,0:T(8,128)(2,1)}), bf16[8,4,320,768]{3,2,1,0:T(8,128)(2,1)}, u32[]{:S(2)}, u32[]{:S(2)}) async-start(bf16[8,4,320,768]{3,2,1,0:T(8,128)(2,1)} %bitcast.44), calls=%async_computation.1 | async-start | bytes 31457280 | tf_op jit(solution)/shard_map/all_to_all | solution.py:51
  765.9 485.0 %all-reduce.4.cloned.1.call-start = ((), (), s32[]{:S(2)}) async-start(), calls=%async_computation.4 | async-start | bytes 196608 | tf_op jit(solution)/shard_map/psum | solution.py:78
  776.4 2004.4 %all-reduce.6.cloned.1.call-start = ((), (), s32[]{:S(2)}) async-start(), calls=%async_computation.5 | async-start | bytes 150994944 | tf_op jit(solution)/shard_map/psum | solution.py:73
  1226.5 178.7 %all-to-all-start.3 = ((bf16[1,4,2560,768]{3,1,0,2:T(4,128)(2,1)}), bf16[1,4,2560,768]{3,1,0,2:T(4,128)(2,1)}, u32[]{:S(2)}, u32[]{:S(2)}) async-start(bf16[1,4,2560,768]{3,1,0,2:T(4,128)(2,1)} %copy.35), calls=%async_computation.3 | async-start | bytes 31457280 | tf_op jit(solution)/shard_map/all_to_all | solution.py:55
  1250.9 169.4 %copy-start.18 = (s32[8192]{0:T(1024)S(1)}, s32[8192]{0:T(1024)}, u32[]{:S(2)}) copy-start(s32[8192]{0:T(1024)} %copy-done.17) | copy-start | bytes 98308
  1252.6 212.4 %copy-start.29 = (f32[768]{0:T(1024)}, f32[768]{0:T(1024)S(1)}, u32[]{:S(2)}) copy-start(f32[768]{0:T(1024)S(1)} %get-tuple-element.23) | copy-start | bytes 9220
  1420.3 44.7 %copy-start.2 = (f32[8192,32]{0,1:T(8,128)S(1)}, f32[8192,32]{0,1:T(8,128)}, u32[]{:S(2)}) copy-start(f32[8192,32]{0,1:T(8,128)} %copy-done.1) | copy-start | bytes 3145732
  1420.3 44.7 %copy-start.6 = (f32[8192]{0:T(1024)S(1)}, f32[8192]{0:T(1024)}, u32[]{:S(2)}) copy-start(f32[8192]{0:T(1024)} %copy-done.5) | copy-start | bytes 98308
  1420.4 44.7 %copy-start.8 = (s32[8192]{0:T(1024)S(1)}, s32[8192]{0:T(1024)}, u32[]{:S(2)}) copy-start(s32[8192]{0:T(1024)} %param.18) | copy-start | bytes 98308
  1420.4 44.7 %copy-start.10 = (f32[8192]{0:T(1024)S(1)}, f32[8192]{0:T(1024)}, u32[]{:S(2)}) copy-start(f32[8192]{0:T(1024)} %copy-done.9) | copy-start | bytes 98308
  1420.4 44.7 %copy-start.12 = (f32[8192]{0:T(1024)S(1)}, f32[8192]{0:T(1024)}, u32[]{:S(2)}) copy-start(f32[8192]{0:T(1024)} %copy-done.11) | copy-start | bytes 98308
  1420.4 44.7 %copy-start.16 = (f32[8192]{0:T(1024)S(1)}, f32[8192]{0:T(1024)}, u32[]{:S(2)}) copy-start(f32[8192]{0:T(1024)} %copy-done.15) | copy-start | bytes 98308
  1420.4 44.7 %copy-start.28 = (pred[8192]{0:T(1024)(128)(4,1)S(1)}, pred[8192]{0:T(1024)(128)(4,1)}, u32[]{:S(2)}) copy-start(pred[8192]{0:T(1024)(128)(4,1)} %get-tuple-element.34) | copy-start | bytes 24580
  (20 other events, 322.3 us)
Sparse Core Ops, SparseCore 0:
  776.5 188.2 all-reduce.3
  1147.1 1633.6 all-reduce.5
where the time goes:
time: 2900 us
  waiting for transfers between devices  1760 us (61%)
  matrix products  432 us (15%)
  local copies, waits for them, and re-layouts  322 us (11%)
  blocking collectives  178 us (6%)
  other arithmetic  169 us (6%)
    psum x1, waiting for transfers between devices, local_step(): grad_win = lax.psum(grad_win, 'dp')  1290 us
    all_to_all x2, waiting for transfers between devices, to_tokens(): lax.all_to_all(expert_rows.reshape(1, experts_local, ep_size * capacity,...  306 us
    all_to_all x1, blocking collectives, to_experts(): recv_buf = lax.all_to_all(send_buf, 'ep', 0, 2, tiled=True)  178 us
    all_to_all x1, waiting for transfers between devices, to_experts(): recv_buf = lax.all_to_all(send_buf, 'ep', 0, 2, tiled=True)  163 us
    gather x2, local copies, waits for them, and re-layouts, to_experts(): send_buf = jnp.take(token_rows, src_tok, axis=0, mode='fill', fill_value=0)  104 us
    gather x2, local copies, waits for them, and re-layouts, to_tokens(): return jnp.take(back_buf, flat_pos, axis=0, mode='fill', fill_value=0)  89.2 us
    dot_general x1, matrix products, local_step(): jnp.einsum('erd,efd->erf', recv_gh, w_out, preferred_element_type=jnp.flo...  73.1 us
    dot_general x1, matrix products, local_step(): jnp.einsum('erd,edf->erf', recv_x, w_in, preferred_element_type=jnp.float32)  69.1 us
  transfers between devices with their start and end apart: 5, of which 4 were waited for; matrix products, arithmetic and copies ran while one was open for 15% of the time, Pallas kernels for 0%

commit v1 on v0

v1 whole, which is shorter than its diff:
```python
import jax
import jax.numpy as jnp
from jax import lax
from jax.sharding import PartitionSpec as P
import math

OPT_STEP = 2
DECAY_RATE = 1.0 - OPT_STEP ** -0.8
LR_BASE = min(0.01, 1.0 / math.sqrt(OPT_STEP))
AUX_COEF = 0.01
PRECISE = lax.Precision.HIGHEST
F32 = jnp.float32
BF16 = jnp.bfloat16


def optimizer_step(weight, gradient, row_stat, col_stat):
    grad_sq = gradient * gradient + 1e-30
    row_new = DECAY_RATE * row_stat + (1.0 - DECAY_RATE) * jnp.mean(grad_sq, axis=-1)
    col_new = DECAY_RATE * col_stat + (1.0 - DECAY_RATE) * jnp.mean(grad_sq, axis=-2)
    row_norm = row_new / jnp.mean(row_new, axis=-1, keepdims=True)
    update = gradient * lax.rsqrt(row_norm)[..., :, None] * lax.rsqrt(col_new)[..., None, :]
    upd_rms = jnp.sqrt(jnp.mean(update * update, axis=(-2, -1), keepdims=True))
    update = update / jnp.maximum(1.0, upd_rms)
    w_full = weight.astype(F32)
    w_rms = jnp.sqrt(jnp.mean(w_full * w_full, axis=(-2, -1), keepdims=True))
    new_weight = w_full - LR_BASE * jnp.maximum(1e-3, w_rms) * update
    return new_weight, row_new, col_new


def split3(value):
    hi = lax.reduce_precision(value, 8, 7)
    rest = value - hi
    mid = lax.reduce_precision(rest, 8, 7)
    lo = rest - mid
    return hi.astype(BF16), mid.astype(BF16), lo.astype(BF16)


def mm(a, b, dims):
    return lax.dot_general(a, b, (dims, ((), ())), preferred_element_type=F32)


def solution(mesh):
    ep_size = mesh.shape['ep']
    dp_size = mesh.shape['dp']
    tok_spec = P(('dp', 'ep'))
    row_spec = P(('dp', 'ep'), None)
    exp_spec = P('ep')
    full_spec = P()
    swap = [(i, (i + 1) % dp_size) for i in range(dp_size)]

    def local_step(x_tokens, expert_id, token_slot, grad_y, w_router, w_in, w_out, row_in, col_in, row_out, col_out, row_router, col_router):
        tokens, width = x_tokens.shape
        el = w_in.shape[0]
        experts = w_router.shape[1]
        cap = 5 * tokens // (4 * experts)
        own = el // dp_size
        zi = lax.axis_index('dp')
        base = own * zi

        is_e = expert_id[:, None] == jnp.arange(experts)[None, :]
        onehot = is_e.astype(F32)
        onehot_b = is_e.astype(BF16)
        is_c = token_slot[:, None] == jnp.arange(cap)[None, :]
        tok_idx = jnp.arange(tokens, dtype=jnp.int32)

        def to_slots(vals):
            cols = jnp.concatenate([jnp.where(is_c, v.astype(BF16)[:, None], jnp.zeros((), BF16)) for v in vals], axis=1)
            out = mm(onehot_b, cols, ((0,), (0,)))
            return [out[:, i * cap:(i + 1) * cap] for i in range(len(vals))]

        t_hi, t_lo, t_cnt = to_slots([tok_idx // 64, tok_idx % 64, jnp.ones_like(tok_idx)])
        src = (t_hi * 64.0 + t_lo).astype(jnp.int32)
        src = jnp.where(t_cnt > 0.5, src, tokens)

        def by_pos(table):
            return jnp.roll(table.reshape(ep_size, el, cap), -base, axis=1)

        src_pos = by_pos(src)

        r_hi, r_mid, r_lo = split3(w_router)
        lg = mm(x_tokens, jnp.concatenate([r_hi, r_mid, r_lo], axis=1), ((1,), (0,)))
        logits = lg[:, :experts] + (lg[:, experts:2 * experts] + lg[:, 2 * experts:])
        gate_probs = jax.nn.softmax(logits, axis=-1)
        gate_val = jnp.sum(gate_probs * onehot, axis=-1)
        p_hi, p_mid, p_lo = to_slots(list(split3(gate_val)))
        p_slot = p_hi + (p_mid + p_lo)
        p_recv = lax.all_to_all(by_pos(p_slot), 'ep', 0, 0, tiled=True)

        def send(rows, q):
            buf = jnp.take(rows, src_pos[:, q].reshape(-1), axis=0, mode='fill', fill_value=0)
            buf = buf.reshape(ep_size, cap, width)
            return lax.all_to_all(buf, 'ep', 0, 0, tiled=True).reshape(ep_size * cap, width)

        def weight(w, q):
            return lax.dynamic_index_in_dim(w, lax.rem(base + q, el), 0, keepdims=False)

        order = []
        for k in range(own):
            order += [own + k, k]
        res = {}
        g_pos, back = {}, {}
        for q in order:
            xq = send(x_tokens, q)
            yq = send(grad_y, q)
            w1, w2 = weight(w_in, q), weight(w_out, q)
            pq = p_recv[:, q].reshape(-1)
            dhq = (pq[:, None] * yq).astype(BF16)
            pre = mm(xq, w1, ((1,), (0,))).astype(BF16)
            act = jnp.maximum(pre, 0)
            h = mm(act, w2, ((1,), (0,))).astype(BF16)
            g_pos[q] = jnp.sum(yq.astype(F32) * h.astype(F32), axis=-1)
            da = jnp.where(pre > 0, mm(dhq, w2, ((1,), (1,))), 0.0).astype(BF16)
            dbuf = mm(da, w1, ((1,), (1,))).astype(BF16)
            back[q] = lax.all_to_all(dbuf.reshape(ep_size, cap, width), 'ep', 0, 0, tiled=True).reshape(ep_size * cap, width)
            res[q] = (xq, dhq, act, da)

        new_in, new_out, stats = [], [], []
        for k in range(own):
            w1, w2 = weight(w_in, k), weight(w_out, k)
            xp = lax.ppermute(res[own + k][0], 'dp', swap)
            dhp = lax.ppermute(res[own + k][1], 'dp', swap)
            pre_p = mm(xp, w1, ((1,), (0,))).astype(BF16)
            act_p = jnp.maximum(pre_p, 0)
            da_p = jnp.where(pre_p > 0, mm(dhp, w2, ((1,), (1,))), 0.0).astype(BF16)
            xq, dhq, act, da = res[k]
            d_out = mm(act, dhq, ((0,), (0,))) + mm(act_p, dhp, ((0,), (0,)))
            d_in = mm(xq, da, ((0,), (0,))) + mm(xp, da_p, ((0,), (0,)))
            no, ro, co = optimizer_step(w2, d_out, weight(row_out, k), weight(col_out, k))
            ni, ri, ci = optimizer_step(w1, d_in, weight(row_in, k), weight(col_in, k))
            new_out.append(no.astype(BF16))
            new_in.append(ni.astype(BF16))
            stats.append((ri, ci, ro, co))

        def assemble(mine, like):
            theirs = [lax.ppermute(m, 'dp', swap) for m in mine]
            out = jnp.zeros((el,) + mine[0].shape, like)
            for k, m in enumerate(mine):
                out = lax.dynamic_update_index_in_dim(out, m, lax.rem(base + k, el), 0)
            for k, m in enumerate(theirs):
                out = lax.dynamic_update_index_in_dim(out, m, lax.rem(base + own + k, el), 0)
            return out

        out_w_out = assemble(new_out, BF16)
        out_w_in = assemble(new_in, BF16)
        out_stats = []
        for i in range(4):
            mine = jnp.stack([s[i] for s in stats])
            both = jnp.concatenate([mine, lax.ppermute(mine, 'dp', swap)], axis=0)
            out_stats.append(jnp.roll(both, base, axis=0))

        g_buf = jnp.stack([g_pos[q].reshape(ep_size, cap) for q in range(el)], axis=1)
        g_back = lax.all_to_all(g_buf, 'ep', 0, 0, tiled=True)
        g_slot = jnp.roll(g_back, base, axis=1).reshape(experts, cap)
        g3 = jnp.concatenate(split3(g_slot), axis=0)
        onehot3 = jnp.concatenate([onehot_b] * 3, axis=1)
        g_rows = mm(onehot3, g3, ((1,), (0,)))
        grad_gate = jnp.sum(jnp.where(is_c, g_rows, 0.0), axis=-1)

        route_frac = jnp.mean(onehot, axis=0)
        grad_prob = onehot * grad_gate[:, None] + AUX_COEF * experts * route_frac[None, :] / tokens
        grad_logits = gate_probs * (grad_prob - jnp.sum(gate_probs * grad_prob, axis=-1, keepdims=True))
        l1, l2, l3 = split3(grad_logits)
        gr = mm(x_tokens, jnp.concatenate([l1, l2, l3], axis=1), ((0,), (0,)))
        grad_router = lax.psum(gr[:, :experts] + (gr[:, experts:2 * experts] + gr[:, 2 * experts:]), ('dp', 'ep'))
        lcat = jnp.concatenate([l1, l1, l2, l1, l2, l3], axis=1)
        wcat = jnp.concatenate([r_hi, r_mid, r_hi, r_lo, r_mid, r_hi], axis=1)
        dx_router = mm(lcat, wcat, ((1,), (1,)))

        back_all = jnp.concatenate([back[q] for q in range(el)], axis=0)
        pos_e = lax.rem(expert_id % el - base + el, el)
        back_pos = jnp.where(token_slot >= 0, (pos_e * ep_size + expert_id // el) * cap + token_slot, experts * cap)
        dx_expert = jnp.take(back_all, back_pos, axis=0, mode='fill', fill_value=0)
        grad_x = (dx_expert.astype(F32) + dx_router).astype(BF16)
        new_router, row_router_new, col_router_new = optimizer_step(w_router, grad_router, row_router, col_router)
        return (out_w_in, out_w_out, new_router, out_stats[0], out_stats[1], out_stats[2], out_stats[3], row_router_new, col_router_new, grad_x)

    in_specs = (row_spec, tok_spec, tok_spec, row_spec, full_spec, exp_spec, exp_spec, exp_spec, exp_spec, exp_spec, exp_spec, full_spec, full_spec)
    out_specs = (exp_spec, exp_spec, full_spec, exp_spec, exp_spec, exp_spec, exp_spec, full_spec, full_spec, row_spec)
    return jax.shard_map(local_step, mesh=mesh, in_specs=in_specs, out_specs=out_specs, check_vma=False)
```

time: 2900 us -> 1620 us (0.56)
  waiting for transfers between devices: 1760 us -> 454 us
  matrix products: 432 us -> 560 us
  blocking collectives: 178 us -> 50.4 us
  local copies, waits for them, and re-layouts: 322 us -> 248 us
  starting transfers between devices: 17.7 us -> 80.6 us
    psum x2 -> x1, waiting for transfers between devices: 1290 us -> 0.01 us  [local_step(): lax.psum(gr[:, :experts] + (gr[:, experts:2 * experts] + gr[:, 2 * expert...]
    all_to_all x3 -> x13, waiting for transfers between devices: 469 us -> 93.5 us  [the longest x7 45.4 us: send(): lax.all_to_all(buf, 'ep', 0, 0, tiled=True).reshape(ep_size * cap, width)]
    ppermute x0 -> x12, waiting for transfers between devices: none -> 360 us  [the longest x4 360 us: local_step(): both = jnp.concatenate([mine, lax.ppermute(mine, 'dp', swap)], axis=0)]
    dot_general x9 -> x30, matrix products: 432 us -> 560 us  [mm(): return lax.dot_general(a, b, (dims, ((), ())), preferred_element_type=F32)]
    all_to_all x1, blocking collectives: 178 us -> 50.4 us  [send(): lax.all_to_all(buf, 'ep', 0, 0, tiled=True).reshape(ep_size * cap, width)]
    all_to_all x4 -> x0, local copies, waits for them, and re-layouts: 49.7 us -> none  [the longest x2 30.3 us: to_tokens(): lax.all_to_all(expert_rows.reshape(1, experts_local, ep_size * capacity,...]
    all_to_all x3 -> x13, starting transfers between devices: 17.6 us -> 62.8 us  [the longest x7 34.8 us: send(): lax.all_to_all(buf, 'ep', 0, 0, tiled=True).reshape(ep_size * cap, width)]
    reshape x2 -> x3, local copies, waits for them, and re-layouts: 42.1 us -> 0.06 us  [the longest x2 0.04 us: by_pos(): return jnp.roll(table.reshape(ep_size, el, cap), -base, axis=1)]
  transfers between devices with their start and end apart: 5 -> 26, of which waited for: 4 -> 12; matrix products, arithmetic and copies ran while one was open for 15% -> 49% of each run, Pallas kernels for 0% -> 0%
where the time goes in v1:
time: 1620 us; the launch traced here: 1610 us
  matrix products  560 us (35%)
  waiting for transfers between devices  454 us (28%)
  local copies, waits for them, and re-layouts  248 us (15%)
  other arithmetic  188 us (12%)
  starting transfers between devices  80.6 us (5%)
  blocking collectives  50.4 us (3%)
  between operations  25.5 us (2%)
    dot_general x30, matrix products, mm(): return lax.dot_general(a, b, (dims, ((), ())), preferred_element_type=F32)  560 us
    ppermute x4, waiting for transfers between devices, local_step(): both = jnp.concatenate([mine, lax.ppermute(mine, 'dp', swap)], axis=0)  360 us
    gather x8, local copies, waits for them, and re-layouts, send(): jnp.take(rows, src_pos[:, q].reshape(-1), axis=0, mode='fill', fill_value=0)  132 us
    all_to_all x1, blocking collectives, send(): lax.all_to_all(buf, 'ep', 0, 0, tiled=True).reshape(ep_size * cap, width)  50.4 us
    all_to_all x7, waiting for transfers between devices, send(): lax.all_to_all(buf, 'ep', 0, 0, tiled=True).reshape(ep_size * cap, width)  45.4 us
    gather x1, local copies, waits for them, and re-layouts, local_step(): dx_expert = jnp.take(back_all, back_pos, axis=0, mode='fill', fill_value=0)  44.5 us
    all_to_all x4, waiting for transfers between devices, local_step(): lax.all_to_all(dbuf.reshape(ep_size, cap, width), 'ep', 0, 0, tiled=True)  44.1 us
    convert_element_type x8, other arithmetic, local_step(): dhq = (pq[:, None] * yq).astype(BF16)  40.5 us
  transfers between devices with their start and end apart: 26, of which 12 were waited for; matrix products, arithmetic and copies ran while one was open for 49% of the time, Pallas kernels for 0%

profile of v1, /device:TPU:0, one launch (start us, length us, event | category | flops | bytes accessed | tf_op | source)
XLA Modules:
  0.0 1606.0 jit_solution(14583377068311012987)
XLA Ops:
  164.2 50.4 %all_to_all.70 = bf16[8,320,768]{2,1,0:T(8,128)(2,1)} all-to-all(bf16[8,320,768]{2,1,0:T(8,128)(2,1)} %bitcast.209), channel_id=1, replica_groups=mesh['dp'=2,'ep'=8] {'ep'}, dimensions={0} | all-to-all | bytes 7864320 | tf_op jit(solution)/shard_map/all_to_all | solution.py:92
  288.2 28.8 %all-to-all-done.8 = bf16[8,320,768]{2,1,0:T(8,128)(2,1)} async-done(((bf16[8,320,768]{2,1,0:T(8,128)(2,1)}), bf16[8,320,768]{2,1,0:T(8,128)(2,1)}, u32[]{:S(2)}, u32[]{:S(2)}) %all-to-all-start.8) | async-done | bytes 3932192 | tf_op jit(solution)/shard_map/all_to_all | solution.py:92
  322.1 18.7 %convolution_convert_fusion.3 = bf16[2560,3072]{1,0:T(8,128)(2,1)} fusion(bf16[2560,768]{1,0:T(8,128)(2,1)} %bitcast.16, bf16[4,768,3072]{2,1,0:T(8,128)(2,1)} %param.26, s32[]{:T(128)S(6)} %select_n.181), kind=kOutput, calls=%fused_computation.19 | convolution fusion | flops 12087459840 | bytes 24379396 | tf_op jit(solution)/shard_map/dot_general | solution.py:39
  406.7 18.8 %multiply_reduce_fusion.4 = f32[2560]{0:T(1024)S(1)} fusion(f32[2560,768]{0,1:T(8,128)} %copy.30, bf16[4,3072,768]{2,1,0:T(8,128)(2,1)} %param.27, s32[]{:T(128)S(6)} %select_n.185, bf16[2560,3072]{1,0:T(8,128)(2,1)} %convolution_convert_fusion), kind=kOutput, calls=%fused_computation.104 | convolution fusion | flops 12095322112 | bytes 28321796 | tf_op jit(solution)/shard_map/dot_general | solution.py:39
  430.4 18.7 %convolution_convert_fusion.1 = bf16[2560,3072]{1,0:T(8,128)(2,1)} fusion(bf16[2560,768]{1,0:T(8,128)(2,1)} %bitcast.8, bf16[4,768,3072]{2,1,0:T(8,128)(2,1)} %param.26, s32[]{:T(128)S(6)} %select_n.184), kind=kOutput, calls=%fused_computation.17 | convolution fusion | flops 12087459840 | bytes 24379396 | tf_op jit(solution)/shard_map/dot_general | solution.py:39
  470.9 18.9 %multiply_reduce_fusion.5 = f32[2560]{0:T(1024)S(1)} fusion(f32[2560,768]{0,1:T(8,128)} %copy.29, bf16[4,3072,768]{2,1,0:T(8,128)(2,1)} %param.27, s32[]{:T(128)S(6)} %select_n.184, bf16[2560,3072]{1,0:T(8,128)(2,1)} %convolution_convert_fusion.1), kind=kOutput, calls=%fused_computation.105 | convolution fusion | flops 12095322112 | bytes 28321796 | tf_op jit(solution)/shard_map/dot_general | solution.py:39
  490.0 18.7 %convolution_convert_fusion.5 = bf16[2560,3072]{1,0:T(8,128)(2,1)} fusion(bf16[2560,768]{1,0:T(8,128)(2,1)} %bitcast.2, bf16[4,768,3072]{2,1,0:T(8,128)(2,1)} %param.26, s32[]{:T(128)S(6)} %select_n.167), kind=kOutput, calls=%fused_computation.21 | convolution fusion | flops 12087459840 | bytes 24379396 | tf_op jit(solution)/shard_map/dot_general | solution.py:39
  575.5 21.4 %select_convert_fusion.5 = bf16[2560,3072]{1,0:T(8,128)(2,1)} fusion(bf16[2560,3072]{1,0:T(8,128)(2,1)} %convolution_convert_fusion.5, bf16[2560,768]{1,0:T(8,128)(2,1)} %bitcast.218, bf16[4,3072,768]{2,1,0:T(8,128)(2,1)} %param.27, s32[]{:T(128)S(6)} %select_n.167), kind=kOutput, calls=%fused_computation.14 | convolution fusion | flops 12103188480 | bytes 40108036 | tf_op jit(solution)/shard_map/dot_general | solution.py:39
  636.1 32.7 %convolution_convert_fusion.6 = bf16[2560,768]{1,0:T(8,128)(2,1)} fusion(bf16[4,768,3072]{2,1,0:T(8,128)(2,1)} %param.26, s32[]{:T(128)S(6)} %select_n.185, bf16[2560,3072]{1,0:T(8,128)(2,1)} %convolution_convert_fusion, bf16[2560,768]{1,0:T(8,128)(2,1)} %bitcast.216, bf16[4,3072,768]{2,1,0:T(8,128)(2,1)} %param.27), kind=kOutput, calls=%fused_computation.132 | convolution fusion | flops 24184750080 | bytes 33031168 | tf_op jit(solution)/shard_map/dot_general | solution.py:39
  678.2 21.2 %select_convert_fusion.3 = bf16[2560,3072]{1,0:T(8,128)(2,1)} fusion(bf16[2560,3072]{1,0:T(8,128)(2,1)} %convolution_convert_fusion.3, bf16[2560,768]{1,0:T(8,128)(2,1)} %bitcast.219, bf16[4,3072,768]{2,1,0:T(8,128)(2,1)} %param.27, s32[]{:T(128)S(6)} %select_n.181), kind=kOutput, calls=%fused_computation.12 | convolution fusion | flops 12103188480 | bytes 40108036 | tf_op jit(solution)/shard_map/dot_general | solution.py:39
  704.1 32.4 %convolution_convert_fusion.7 = bf16[2560,768]{1,0:T(8,128)(2,1)} fusion(bf16[4,768,3072]{2,1,0:T(8,128)(2,1)} %param.26, s32[]{:T(128)S(6)} %select_n.184, bf16[2560,3072]{1,0:T(8,128)(2,1)} %convolution_convert_fusion.1, bf16[2560,768]{1,0:T(8,128)(2,1)} %bitcast.217, bf16[4,3072,768]{2,1,0:T(8,128)(2,1)} %param.27), kind=kOutput, calls=%fused_computation.133 | convolution fusion | flops 24184750080 | bytes 33031168 | tf_op jit(solution)/shard_map/dot_general | solution.py:39
  798.9 19.1 %fusion.26 = f32[3072,768]{1,0:T(8,128)} fusion(bf16[2560,3072]{1,0:T(8,128)(2,1)} %convolution_convert_fusion.3, f32[2560]{0:T(1024)S(1)} %mul.602, bf16[2560,768]{1,0:T(8,128)(2,1)} %bitcast.199), kind=kOutput, calls=%fused_computation.49 | convolution fusion | flops 12093358080 | bytes 29108224 | tf_op jit(solution)/shard_map/dot_general | solution.py:39
  817.9 20.7 %all-to-all-done.10 = bf16[8,320,768]{2,1,0:T(8,128)(2,1)} async-done(((bf16[8,320,768]{2,1,0:T(8,128)(2,1)}), bf16[8,320,768]{2,1,0:T(8,128)(2,1)}, u32[]{:S(2)}, u32[]{:S(2)}) %all-to-all-start.10) | async-done | bytes 3932192 | tf_op jit(solution)/shard_map/all_to_all | solution.py:114
  843.7 19.2 %fusion.30 = f32[3072,768]{1,0:T(8,128)} fusion(bf16[2560,3072]{1,0:T(8,128)(2,1)} %convolution_convert_fusion.5, f32[2560]{0:T(1024)S(1)} %mul.582, bf16[2560,768]{1,0:T(8,128)(2,1)} %bitcast.132), kind=kOutput, calls=%fused_computation.53 | convolution fusion | flops 12093358080 | bytes 29108224 | tf_op jit(solution)/shard_map/dot_general | solution.py:39
  869.7 20.2 %all-to-all-done.11 = bf16[8,320,768]{2,1,0:T(8,128)(2,1)} async-done(((bf16[8,320,768]{2,1,0:T(8,128)(2,1)}), bf16[8,320,768]{2,1,0:T(8,128)(2,1)}, u32[]{:S(2)}, u32[]{:S(2)}) %all-to-all-start.11) | async-done | bytes 3932192 | tf_op jit(solution)/shard_map/all_to_all | solution.py:114
  889.9 20.6 %pad_maximum_fusion = bf16[10240,768]{1,0:T(8,128)(2,1)} fusion(bf16[2560,768]{1,0:T(8,128)(2,1)} %bitcast.53, bf16[2560,768]{1,0:T(8,128)(2,1)} %bitcast.50, bf16[2560,768]{1,0:T(8,128)(2,1)} %bitcast.47, bf16[2560,768]{1,0:T(8,128)(2,1)} %bitcast.45), kind=kLoop, calls=%fused_computation.36 | loop fusion | flops 62914560 | bytes 31457280 | tf_op jit(solution)/shard_map/concatenate | solution.py:169
  910.5 44.5 %gather_fusion = bf16[8192,768]{1,0:T(8,128)(2,1)} fusion(bf16[10240,768]{1,0:T(8,128)(2,1)} %pad_maximum_fusion, s32[8192]{0:T(1024)S(1)} %copy-done.17), kind=kCustom, calls=%fused_computation.8 | custom fusion | bytes 25198592 | tf_op jit(solution)/shard_map/jit(_take)/gather | solution.py:172
  955.1 18.8 %convolution_convert_fusion.4 = bf16[2560,3072]{1,0:T(8,128)(2,1)} fusion(bf16[2560,768]{1,0:T(8,128)(2,1)} %collective-permute-done, bf16[4,768,3072]{2,1,0:T(8,128)(2,1)} %param.26, s32[]{:T(128)S(6)} %select_n.167), kind=kOutput, calls=%fused_computation.20 | convolution fusion | flops 12087459840 | bytes 24379396 | tf_op jit(solution)/shard_map/dot_general | solution.py:39
  973.9 18.7 %convolution_convert_fusion.2 = bf16[2560,3072]{1,0:T(8,128)(2,1)} fusion(bf16[2560,768]{1,0:T(8,128)(2,1)} %collective-permute-done.2, bf16[4,768,3072]{2,1,0:T(8,128)(2,1)} %param.26, s32[]{:T(128)S(6)} %select_n.181), kind=kOutput, calls=%fused_computation.18 | convolution fusion | flops 12087459840 | bytes 24379396 | tf_op jit(solution)/shard_map/dot_general | solution.py:39
  992.6 21.8 %fusion.55 = (f32[3072]{0:T(1024)S(1)}, f32[768]{0:T(1024)S(1)}, f32[3072,768]{1,0:T(8,128)}) fusion(f32[3072,768]{1,0:T(8,128)} %fusion.30, bf16[2560,768]{1,0:T(8,128)(2,1)} %collective-permute-done.1, bf16[2560,3072]{1,0:T(8,128)(2,1)} %convolution_convert_fusion.4), kind=kOutput, calls=%fused_computation.99 | convolution fusion | flops 12099252224 | bytes 38550528 | tf_op jit(solution)/shard_map/dot_general | solution.py:39
  1014.4 37.4 %fusion.51 = (f32[768]{0:T(1024)S(1)}, f32[3072]{0:T(1024)S(1)}, f32[768,3072]{1,0:T(8,128)}) fusion(f32[768,3072]{1,0:T(8,128)} %fusion.324, bf16[2560,768]{1,0:T(8,128)(2,1)} %collective-permute-done, bf16[2560,3072]{1,0:T(8,128)(2,1)} %convolution_convert_fusion.4, bf16[2560,768]{1,0:T(8,128)(2,1)} %collective-permute-done.1, ...), kind=kOutput, calls=%fused_computation.95 | convolution fusion | flops 24194576384 | bytes 47201284 | tf_op jit(solution)/shard_map/dot_general | solution.py:39
  1051.8 37.7 %fusion.53 = (f32[768]{0:T(1024)S(1)}, f32[3072]{0:T(1024)S(1)}, f32[768,3072]{1,0:T(8,128)}) fusion(f32[768,3072]{1,0:T(8,128)} %fusion.325, bf16[2560,768]{1,0:T(8,128)(2,1)} %collective-permute-done.2, bf16[2560,3072]{1,0:T(8,128)(2,1)} %convolution_convert_fusion.2, bf16[2560,768]{1,0:T(8,128)(2,1)} %collective-permute-done.3, ...), kind=kOutput, calls=%fused_computation.97 | convolution fusion | flops 24194576384 | bytes 47201284 | tf_op jit(solution)/shard_map/dot_general | solution.py:39
  1089.5 21.8 %fusion.57 = (f32[3072]{0:T(1024)S(1)}, f32[768]{0:T(1024)S(1)}, f32[3072,768]{1,0:T(8,128)}) fusion(f32[3072,768]{1,0:T(8,128)} %fusion.26, bf16[2560,768]{1,0:T(8,128)(2,1)} %collective-permute-done.3, bf16[2560,3072]{1,0:T(8,128)(2,1)} %convolution_convert_fusion.2), kind=kOutput, calls=%fused_computation.101 | convolution fusion | flops 12099252224 | bytes 38550528 | tf_op jit(solution)/shard_map/dot_general | solution.py:39
  1211.6 355.9 %collective-permute-done.11 = f32[2,768]{1,0:T(2,128)S(1)} collective-permute-done((f32[2,768]{1,0:T(2,128)S(1)}, f32[2,768]{1,0:T(2,128)S(1)}, u32[]{:S(2)}, u32[]{:S(2)}) %collective-permute-start.11) | collective-permute-done | bytes 6176 | tf_op jit(solution)/shard_map/ppermute | solution.py:148
  (304 shorter events, 643.4 us)
Async XLA Ops:
  61.1 52.2 %all-to-all-start.2 = ((bf16[8,320,768]{2,1,0:T(8,128)(2,1)}), bf16[8,320,768]{2,1,0:T(8,128)(2,1)}, u32[]{:S(2)}, u32[]{:S(2)}) async-start(bf16[8,320,768]{2,1,0:T(8,128)(2,1)} %bitcast.208), calls=%async_computation.2 | async-start | bytes 7864320 | tf_op jit(solution)/shard_map/all_to_all | solution.py:92
  113.3 50.9 %all-to-all-start.4 = ((bf16[8,320,768]{2,1,0:T(8,128)(2,1)}), bf16[8,320,768]{2,1,0:T(8,128)(2,1)}, u32[]{:S(2)}, u32[]{:S(2)}) async-start(bf16[8,320,768]{2,1,0:T(8,128)(2,1)} %bitcast.207), calls=%async_computation.4 | async-start | bytes 7864320 | tf_op jit(solution)/shard_map/all_to_all | solution.py:92
  214.6 51.4 %all-to-all-start.5 = ((bf16[8,320,768]{2,1,0:T(8,128)(2,1)}), bf16[8,320,768]{2,1,0:T(8,128)(2,1)}, u32[]{:S(2)}, u32[]{:S(2)}) async-start(bf16[8,320,768]{2,1,0:T(8,128)(2,1)} %bitcast.206), calls=%async_computation.5 | async-start | bytes 7864320 | tf_op jit(solution)/shard_map/all_to_all | solution.py:92
  266.0 51.0 %all-to-all-start.8 = ((bf16[8,320,768]{2,1,0:T(8,128)(2,1)}), bf16[8,320,768]{2,1,0:T(8,128)(2,1)}, u32[]{:S(2)}, u32[]{:S(2)}) async-start(bf16[8,320,768]{2,1,0:T(8,128)(2,1)} %bitcast.205), calls=%async_computation.8 | async-start | bytes 7864320 | tf_op jit(solution)/shard_map/all_to_all | solution.py:92
  317.0 51.2 %all-to-all-start.7 = ((bf16[8,320,768]{2,1,0:T(8,128)(2,1)}), bf16[8,320,768]{2,1,0:T(8,128)(2,1)}, u32[]{:S(2)}, u32[]{:S(2)}) async-start(bf16[8,320,768]{2,1,0:T(8,128)(2,1)} %bitcast.204), calls=%async_computation.7 | async-start | bytes 7864320 | tf_op jit(solution)/shard_map/all_to_all | solution.py:92
  368.2 57.3 %all-to-all-start.3 = ((bf16[8,320,768]{2,1,0:T(8,128)(2,1)}), bf16[8,320,768]{2,1,0:T(8,128)(2,1)}, u32[]{:S(2)}, u32[]{:S(2)}) async-start(bf16[8,320,768]{2,1,0:T(8,128)(2,1)} %bitcast.203), calls=%async_computation.3 | async-start | bytes 7864320 | tf_op jit(solution)/shard_map/all_to_all | solution.py:92
  425.5 64.4 %all-to-all-start = ((bf16[8,320,768]{2,1,0:T(8,128)(2,1)}), bf16[8,320,768]{2,1,0:T(8,128)(2,1)}, u32[]{:S(2)}, u32[]{:S(2)}) async-start(bf16[8,320,768]{2,1,0:T(8,128)(2,1)} %bitcast.202), calls=%async_computation | async-start | bytes 7864320 | tf_op jit(solution)/shard_map/all_to_all | solution.py:92
  528.1 10.6 all-to-all-start.9
  536.4 437.5 %collective-permute-start.2 = (bf16[2560,768]{1,0:T(8,128)(2,1)}, bf16[2560,768]{1,0:T(8,128)(2,1)}, u32[]{:S(2)}, u32[]{:S(2)}) collective-permute-start(bf16[2560,768]{1,0:T(8,128)(2,1)} %bitcast.21), channel_id=1, source_target_pairs={{0,8},{8,0},{1,9},{9,1},{2,10},{10,2},{3,11},{11,3},{4,12},{12,4},... | collective-permute-start | bytes 11796488 | tf_op jit(solution)/shard_map/ppermute | solution.py:120
  538.6 416.4 %collective-permute-start = (bf16[2560,768]{1,0:T(8,128)(2,1)}, bf16[2560,768]{1,0:T(8,128)(2,1)}, u32[]{:S(2)}, u32[]{:S(2)}) collective-permute-start(bf16[2560,768]{1,0:T(8,128)(2,1)} %bitcast.8), channel_id=1, source_target_pairs={{0,8},{8,0},{1,9},{9,1},{2,10},{10,2},{3,11},{11,3},{4,12},{12,4},... | collective-permute-start | bytes 11796488 | tf_op jit(solution)/shard_map/ppermute | solution.py:120
  561.1 8.9 all-to-all-start.1
  565.3 297.7 %all-reduce.2.cloned.1.call-start = ((), (), s32[]{:S(2)}) async-start(), calls=%async_computation.14 | async-start | bytes 196608 | tf_op jit(solution)/shard_map/psum | solution.py:164
  668.7 67.8 %all-to-all-start.13 = ((bf16[8,320,768]{2,1,0:T(8,128)(2,1)}), bf16[8,320,768]{2,1,0:T(8,128)(2,1)}, u32[]{:S(2)}, u32[]{:S(2)}) async-start(bf16[8,320,768]{2,1,0:T(8,128)(2,1)} %bitcast.215), calls=%async_computation.13 | async-start | bytes 7864320 | tf_op jit(solution)/shard_map/all_to_all | solution.py:114
  736.6 51.0 %all-to-all-start.12 = ((bf16[8,320,768]{2,1,0:T(8,128)(2,1)}), bf16[8,320,768]{2,1,0:T(8,128)(2,1)}, u32[]{:S(2)}, u32[]{:S(2)}) async-start(bf16[8,320,768]{2,1,0:T(8,128)(2,1)} %bitcast.214), calls=%async_computation.12 | async-start | bytes 7864320 | tf_op jit(solution)/shard_map/all_to_all | solution.py:114
  764.8 227.8 %collective-permute-start.1 = (bf16[2560,768]{1,0:T(8,128)(2,1)}, bf16[2560,768]{1,0:T(8,128)(2,1)}, u32[]{:S(2)}, u32[]{:S(2)}) collective-permute-start(bf16[2560,768]{1,0:T(8,128)(2,1)} %multiply_convert_fusion.6), channel_id=1, source_target_pairs={{0,8},{8,0},{1,9},{9,1},{2,10},{10,2},{3,11},{11,3},{4,12},{12,4},... | collective-permute-start | bytes 11796488 | tf_op jit(solution)/shard_map/ppermute | solution.py:121
  787.5 51.1 %all-to-all-start.10 = ((bf16[8,320,768]{2,1,0:T(8,128)(2,1)}), bf16[8,320,768]{2,1,0:T(8,128)(2,1)}, u32[]{:S(2)}, u32[]{:S(2)}) async-start(bf16[8,320,768]{2,1,0:T(8,128)(2,1)} %bitcast.212), calls=%async_computation.10 | async-start | bytes 7864320 | tf_op jit(solution)/shard_map/all_to_all | solution.py:114
  797.2 254.7 %collective-permute-start.3 = (bf16[2560,768]{1,0:T(8,128)(2,1)}, bf16[2560,768]{1,0:T(8,128)(2,1)}, u32[]{:S(2)}, u32[]{:S(2)}) collective-permute-start(bf16[2560,768]{1,0:T(8,128)(2,1)} %multiply_convert_fusion.4), channel_id=1, source_target_pairs={{0,8},{8,0},{1,9},{9,1},{2,10},{10,2},{3,11},{11,3},{4,12},{12,4},... | collective-permute-start | bytes 11796488 | tf_op jit(solution)/shard_map/ppermute | solution.py:121
  838.6 51.3 %all-to-all-start.11 = ((bf16[8,320,768]{2,1,0:T(8,128)(2,1)}), bf16[8,320,768]{2,1,0:T(8,128)(2,1)}, u32[]{:S(2)}, u32[]{:S(2)}) async-start(bf16[8,320,768]{2,1,0:T(8,128)(2,1)} %bitcast.213), calls=%async_computation.11 | async-start | bytes 7864320 | tf_op jit(solution)/shard_map/all_to_all | solution.py:114
  1163.6 420.8 %collective-permute-start.7 = (bf16[3072,768]{1,0:T(8,128)(2,1)}, bf16[3072,768]{1,0:T(8,128)(2,1)}, u32[]{:S(2)}, u32[]{:S(2)}) collective-permute-start(bf16[3072,768]{1,0:T(8,128)(2,1)} %get-tuple-element.63), channel_id=1, source_target_pairs={{0,8},{8,0},{1,9},{9,1},{2,10},{10,2},{3,11},{11,3},{4,12},{12,4},... | collective-permute-start | bytes 14155784 | tf_op jit(solution)/shard_map/ppermute | solution.py:135
  1171.4 408.2 %collective-permute-start.6 = (bf16[3072,768]{1,0:T(8,128)(2,1)}, bf16[3072,768]{1,0:T(8,128)(2,1)}, u32[]{:S(2)}, u32[]{:S(2)}) collective-permute-start(bf16[3072,768]{1,0:T(8,128)(2,1)} %get-tuple-element.67), channel_id=1, source_target_pairs={{0,8},{8,0},{1,9},{9,1},{2,10},{10,2},{3,11},{11,3},{4,12},{12,4},... | collective-permute-start | bytes 14155784 | tf_op jit(solution)/shard_map/ppermute | solution.py:135
  1198.9 395.2 %collective-permute-start.5 = (bf16[768,3072]{1,0:T(8,128)(2,1)}, bf16[768,3072]{1,0:T(8,128)(2,1)}, u32[]{:S(2)}, u32[]{:S(2)}) collective-permute-start(bf16[768,3072]{1,0:T(8,128)(2,1)} %get-tuple-element.71), channel_id=1, source_target_pairs={{0,8},{8,0},{1,9},{9,1},{2,10},{10,2},{3,11},{11,3},{4,12},{12,4},... | collective-permute-start | bytes 14155784 | tf_op jit(solution)/shard_map/ppermute | solution.py:135
  1200.4 388.8 %collective-permute-start.4 = (bf16[768,3072]{1,0:T(8,128)(2,1)}, bf16[768,3072]{1,0:T(8,128)(2,1)}, u32[]{:S(2)}, u32[]{:S(2)}) collective-permute-start(bf16[768,3072]{1,0:T(8,128)(2,1)} %get-tuple-element.75), channel_id=1, source_target_pairs={{0,8},{8,0},{1,9},{9,1},{2,10},{10,2},{3,11},{11,3},{4,12},{12,4},... | collective-permute-start | bytes 14155784 | tf_op jit(solution)/shard_map/ppermute | solution.py:135
  1209.9 357.6 %collective-permute-start.11 = (f32[2,768]{1,0:T(2,128)S(1)}, f32[2,768]{1,0:T(2,128)S(1)}, u32[]{:S(2)}, u32[]{:S(2)}) collective-permute-start(f32[2,768]{1,0:T(2,128)S(1)} %pad_maximum_fusion.5), channel_id=1, source_target_pairs={{0,8},{8,0},{1,9},{9,1},{2,10},{10,2},{3,11},{11,3},{4,12},{12,4},... | collective-permute-start | bytes 18440 | tf_op jit(solution)/shard_map/ppermute | solution.py:148
  1571.1 3.8 collective-permute-start.9
  (52 other events, 700.7 us)
Sparse Core Ops, SparseCore 0:
  570.8 67.0 all-reduce.1

commit v2 on v1

--- a/solution.py
+++ b/solution.py
@@ -1,16 +1,225 @@
+import functools
+import math
+
 import jax
 import jax.numpy as jnp
 from jax import lax
+from jax.experimental import pallas as pl
+from jax.experimental.pallas import tpu as pltpu
 from jax.sharding import PartitionSpec as P
-import math
 
 OPT_STEP = 2
 DECAY_RATE = 1.0 - OPT_STEP ** -0.8
 LR_BASE = min(0.01, 1.0 / math.sqrt(OPT_STEP))
 AUX_COEF = 0.01
-PRECISE = lax.Precision.HIGHEST
 F32 = jnp.float32
 BF16 = jnp.bfloat16
+ROW_BLOCK = 640
+F_CHUNK = 512
+G_CHUNK = 64
+
+
+def kdot(a, b, ca, cb):
+    return lax.dot_general(a, b, (((ca,), (cb,)), ((), ())), preferred_element_type=F32)
+
+
+def adafactor_tile(acc, sub_old, lane_old, sub_new_ref, lane_new_ref, lane_sum, row_is_sub):
+    rows, cols = acc.shape
+    lane_sum[...] = jnp.zeros_like(lane_sum)
+
+    @pl.loop(0, rows // G_CHUNK)
+    def _(i):
+        at = pl.ds(pl.multiple_of(i * G_CHUNK, G_CHUNK), G_CHUNK)
+        g = acc[at, :]
+        v = g * g + 1e-30
+        sub_new_ref[at, :] = DECAY_RATE * sub_old[at, :] + (1.0 - DECAY_RATE) * (jnp.sum(v, axis=1, keepdims=True) * (1.0 / cols))
+        lane_sum[...] += jnp.sum(v.reshape(G_CHUNK // 8, 8, cols), axis=0)
+
+    lane_new = DECAY_RATE * lane_old[...] + (1.0 - DECAY_RATE) * (jnp.sum(lane_sum[...], axis=0, keepdims=True) * (1.0 / rows))
+    lane_new_ref[...] = lane_new
+    sub_new = sub_new_ref[...]
+    if row_is_sub:
+        sub_f = lax.rsqrt(sub_new / (jnp.sum(sub_new, axis=0, keepdims=True) * (1.0 / rows)))
+        lane_f = lax.rsqrt(lane_new)
+    else:
+        lane_f = lax.rsqrt(lane_new / (jnp.sum(lane_new, axis=1, keepdims=True) * (1.0 / cols)))
+        sub_f = lax.rsqrt(sub_new)
+    return sub_f, lane_f
+
+
+def expert_kernel(opt, own_blocks, ids, *refs):
+    if opt:
+        (x_own, y_own, p_own, x_par, y_par, p_par, w_in, w_out, sub_in, lane_in, sub_out, lane_out, full_in_i, full_out_i,
+         dbuf, g_out, new_in, new_out, full_in, full_out, sub_in_n, lane_in_n, sub_out_n, lane_out_n,
+         w1, w2, sems, h_acc, b_acc, acc_in, acc_out, sub_f, lane_sum) = refs
+    else:
+        (x_own, y_own, p_own, w_in, w_out, dbuf, g_out, w1, w2, sems, h_acc, b_acc) = refs
+    step = pl.program_id(0)
+    width, ff = w1.shape
+    chunks = ff // F_CHUNK
+
+    @pl.when(step == 0)
+    def _():
+        c1 = pltpu.make_async_copy(w_in.at[ids[0]], w1, sems.at[0])
+        c2 = pltpu.make_async_copy(w_out.at[ids[0]], w2, sems.at[1])
+        c1.start()
+        c2.start()
+        c1.wait()
+        c2.wait()
+        if opt:
+            acc_in[...] = jnp.zeros_like(acc_in)
+            acc_out[...] = jnp.zeros_like(acc_out)
+
+    def body(x_ref, y_ref, p_ref, own):
+        x = x_ref[...]
+        y = y_ref[...].astype(F32)
+        dh = (p_ref[...] * y).astype(BF16)
+        if opt:
+            x_t = x.T
+            dh_t = dh.T
+        if own:
+            h_acc[...] = jnp.zeros_like(h_acc)
+            b_acc[...] = jnp.zeros_like(b_acc)
+
+        @pl.loop(0, chunks)
+        def _(c):
+            at = pl.ds(pl.multiple_of(c * F_CHUNK, F_CHUNK), F_CHUNK)
+            w1c = w1[:, at]
+            w2c = w2[at, :]
+            act = jnp.maximum(kdot(x, w1c, 1, 0).astype(BF16), 0)
+            ga = kdot(dh, w2c, 1, 1)
+            da = jnp.where(act.astype(F32) > 0, ga, 0.0).astype(BF16)
+            if own:
+                h_acc[...] += kdot(act, w2c, 1, 0)
+                b_acc[...] += kdot(da, w1c, 1, 1)
+            if opt:
+                acc_in[:, at] += kdot(x_t, da, 1, 0)
+                acc_out[:, at] += kdot(dh_t, act, 1, 0)
+
+        if own:
+            h = h_acc[...].astype(BF16).astype(F32)
+            g_out[...] = jnp.sum(y_ref[...].astype(F32) * h, axis=1, keepdims=True)
+            dbuf[...] = b_acc[...].astype(BF16)
+
+    if opt:
+        @pl.when(step < own_blocks)
+        def _():
+            body(x_own, y_own, p_own, True)
+
+        @pl.when(step >= own_blocks)
+        def _():
+            body(x_par, y_par, p_par, False)
+
+        @pl.when(step == pl.num_programs(0) - 1)
+        def _():
+            n = float(width * ff)
+
+            def w_scale(w):
+                rows = w.shape[0]
+
+                def one(i, tot):
+                    t = w[pl.ds(pl.multiple_of(i * G_CHUNK, G_CHUNK), G_CHUNK), :].astype(F32)
+                    return tot + jnp.sum(jnp.sum(t * t, axis=1, keepdims=True), axis=0, keepdims=True)
+                tot = lax.fori_loop(0, rows // G_CHUNK, one, jnp.zeros((1, 1), F32))
+                return LR_BASE * jnp.maximum(1e-3, jnp.sqrt(tot * (1.0 / n)))
+
+            def u_scale(acc, lane_f):
+                def one(i, tot):
+                    at = pl.ds(pl.multiple_of(i * G_CHUNK, G_CHUNK), G_CHUNK)
+                    u = acc[at, :] * sub_f[at, :] * lane_f
+                    acc[at, :] = u
+                    return tot + jnp.sum(jnp.sum(u * u, axis=1, keepdims=True), axis=0, keepdims=True)
+                tot = lax.fori_loop(0, width // G_CHUNK, one, jnp.zeros((1, 1), F32))
+                return 1.0 / jnp.maximum(1.0, jnp.sqrt(tot * (1.0 / n)))
+
+            sf, lf = adafactor_tile(acc_in, sub_in, lane_in, sub_in_n, lane_in_n, lane_sum, True)
+            sub_f[...] = sf
+            scale = u_scale(acc_in, lf) * w_scale(w1)
+
+            @pl.loop(0, width // G_CHUNK)
+            def _(i):
+                at = pl.ds(pl.multiple_of(i * G_CHUNK, G_CHUNK), G_CHUNK)
+                w1[at, :] = (w1[at, :].astype(F32) - scale * acc_in[at, :]).astype(BF16)
+
+            o1 = pltpu.make_async_copy(w1, new_in, sems.at[0])
+            o2 = pltpu.make_async_copy(w1, full_in.at[ids[0]], sems.at[1])
+            o1.start()
+            o2.start()
+
+            sf2, lf2 = adafactor_tile(acc_out, sub_out, lane_out, sub_out_n, lane_out_n, lane_sum, False)
+            sub_f[...] = sf2
+            scale2 = u_scale(acc_out, lf2) * w_scale(w2)
+            tc = 256
+
+            @pl.loop(0, ff // tc)
+            def _(i):
+                at = pl.ds(pl.multiple_of(i * tc, tc), tc)
+                w2[at, :] = (w2[at, :].astype(F32) - scale2 * acc_out[:, at].T).astype(BF16)
+
+            o3 = pltpu.make_async_copy(w2, new_out, sems.at[2])
+            o4 = pltpu.make_async_copy(w2, full_out.at[ids[0]], sems.at[3])
+            o3.start()
+            o4.start()
+            o1.wait()
+            o2.wait()
+            o3.wait()
+            o4.wait()
+    else:
+        body(x_own, y_own, p_own, True)
+
+
+def expert_call(eid, x, y, p, w_in, w_out, partner=None, stats=None, full=None):
+    opt = partner is not None
+    rows, width = x.shape
+    el, _, ff = w_in.shape
+    nb = rows // ROW_BLOCK
+    steps = 2 * nb if opt else nb
+    own_map = lambda i, ids: (jnp.minimum(i, nb - 1), 0)
+    par_map = lambda i, ids: (jnp.maximum(i - nb, 0), 0)
+    fixed = lambda i, ids: (0, 0)
+    any_spec = pl.BlockSpec(memory_space=pl.ANY)
+
+    def row_specs(m):
+        return [pl.BlockSpec((ROW_BLOCK, width), m), pl.BlockSpec((ROW_BLOCK, width), m), pl.BlockSpec((ROW_BLOCK, 1), m)]
+
+    in_specs = row_specs(own_map)
+    args = [x, y, p]
+    if opt:
+        in_specs += row_specs(par_map)
+        args += list(partner)
+    in_specs += [any_spec, any_spec]
+    args += [w_in, w_out]
+    out_shape = [jax.ShapeDtypeStruct((rows, width), BF16), jax.ShapeDtypeStruct((rows, 1), F32)]
+    out_specs = [pl.BlockSpec((ROW_BLOCK, width), own_map), pl.BlockSpec((ROW_BLOCK, 1), own_map)]
+    scratch = [pltpu.VMEM((width, ff), BF16), pltpu.VMEM((ff, width), BF16), pltpu.SemaphoreType.DMA((4,)),
+               pltpu.VMEM((ROW_BLOCK, width), F32), pltpu.VMEM((ROW_BLOCK, width), F32)]
+    aliases = {}
+    units = 4
+    if opt:
+        units = 10
+        sub = pl.BlockSpec((width, 1), fixed)
+        lane = pl.BlockSpec((1, ff), fixed)
+        in_specs += [sub, lane, sub, lane, any_spec, any_spec]
+        args += list(stats)
+        if full is None:
+            full = (jnp.zeros((8, 128), BF16), jnp.zeros((8, 128), BF16))
+        else:
+            aliases = {1 + len(args): 4, 2 + len(args): 5}
+        args += list(full)
+        s, l = jax.ShapeDtypeStruct((width, 1), F32), jax.ShapeDtypeStruct((1, ff), F32)
+        out_shape += [jax.ShapeDtypeStruct((width, ff), BF16), jax.ShapeDtypeStruct((ff, width), BF16),
+                      jax.ShapeDtypeStruct(w_in.shape, BF16), jax.ShapeDtypeStruct(w_out.shape, BF16), s, l, s, l]
+        out_specs += [any_spec] * 4 + [sub, lane, sub, lane]
+        scratch += [pltpu.VMEM((width, ff), F32), pltpu.VMEM((width, ff), F32), pltpu.VMEM((width, 1), F32), pltpu.VMEM((8, ff), F32)]
+    return pl.pallas_call(
+        functools.partial(expert_kernel, opt, nb),
+        grid_spec=pltpu.PrefetchScalarGridSpec(num_scalar_prefetch=1, grid=(steps,), in_specs=in_specs, out_specs=out_specs, scratch_shapes=scratch),
+        out_shape=out_shape,
+        input_output_aliases=aliases,
+        compiler_params=pltpu.CompilerParams(dimension_semantics=('arbitrary',), vmem_limit_bytes=64_000_000),
+        cost_estimate=pl.CostEstimate(flops=units * 2 * rows * width * ff, bytes_accessed=4 * rows * width * 2 + 4 * width * ff, transcendentals=0),
+        name='expert_opt' if opt else 'expert_rows',
+    )(eid, *args)
 
 
 def optimizer_step(weight, gradient, row_stat, col_stat):
@@ -85,68 +294,61 @@
         p_hi, p_mid, p_lo = to_slots(list(split3(gate_val)))
         p_slot = p_hi + (p_mid + p_lo)
         p_recv = lax.all_to_all(by_pos(p_slot), 'ep', 0, 0, tiled=True)
+        p_rows = jnp.swapaxes(p_recv, 0, 1).reshape(el, ep_size * cap, 1)
+        p_part = lax.ppermute(p_rows[own:].reshape(own, ep_size * cap), 'dp', swap).reshape(own, ep_size * cap, 1)
 
         def send(rows, q):
             buf = jnp.take(rows, src_pos[:, q].reshape(-1), axis=0, mode='fill', fill_value=0)
             buf = buf.reshape(ep_size, cap, width)
             return lax.all_to_all(buf, 'ep', 0, 0, tiled=True).reshape(ep_size * cap, width)
 
-        def weight(w, q):
-            return lax.dynamic_index_in_dim(w, lax.rem(base + q, el), 0, keepdims=False)
+        def place(q):
+            return lax.rem(base + q, el)
 
         order = []
         for k in range(own):
             order += [own + k, k]
-        res = {}
-        g_pos, back = {}, {}
+        xs, ys, xp, yp = {}, {}, {}, {}
         for q in order:
-            xq = send(x_tokens, q)
-            yq = send(grad_y, q)
-            w1, w2 = weight(w_in, q), weight(w_out, q)
-            pq = p_recv[:, q].reshape(-1)
-            dhq = (pq[:, None] * yq).astype(BF16)
-            pre = mm(xq, w1, ((1,), (0,))).astype(BF16)
-            act = jnp.maximum(pre, 0)
-            h = mm(act, w2, ((1,), (0,))).astype(BF16)
-            g_pos[q] = jnp.sum(yq.astype(F32) * h.astype(F32), axis=-1)
-            da = jnp.where(pre > 0, mm(dhq, w2, ((1,), (1,))), 0.0).astype(BF16)
-            dbuf = mm(da, w1, ((1,), (1,))).astype(BF16)
+            xs[q] = send(x_tokens, q)
+            if q >= own:
+                xp[q - own] = lax.ppermute(xs[q], 'dp', swap)
+            ys[q] = send(grad_y, q)
+            if q >= own:
+                yp[q - own] = lax.ppermute(ys[q], 'dp', swap)
+
+        g_pos, back, new_in, new_out, stats = {}, {}, [], [], []
+        full = None
+        for q in order:
+            eid = place(q).reshape(1)
+            if q >= own:
+                dbuf, g_pos[q] = expert_call(eid, xs[q], ys[q], p_rows[q], w_in, w_out)
+            else:
+                st = (lax.dynamic_index_in_dim(row_in, place(q), 0, keepdims=False)[:, None],
+                      lax.dynamic_index_in_dim(col_in, place(q), 0),
+                      lax.dynamic_index_in_dim(col_out, place(q), 0, keepdims=False)[:, None],
+                      lax.dynamic_index_in_dim(row_out, place(q), 0))
+                dbuf, g_pos[q], ni, no, fi, fo, s_in, l_in, s_out, l_out = expert_call(
+                    eid, xs[q], ys[q], p_rows[q], w_in, w_out, (xp[q], yp[q], p_part[q]), st, full)
+                full = (fi, fo)
+                new_in.append(lax.ppermute(ni, 'dp', swap))
+                new_out.append(lax.ppermute(no, 'dp', swap))
+                stats.append((s_in[:, 0], l_in[0], l_out[0], s_out[:, 0]))
             back[q] = lax.all_to_all(dbuf.reshape(ep_size, cap, width), 'ep', 0, 0, tiled=True).reshape(ep_size * cap, width)
-            res[q] = (xq, dhq, act, da)
-
-        new_in, new_out, stats = [], [], []
+
+        out_w_in, out_w_out = full
         for k in range(own):
-            w1, w2 = weight(w_in, k), weight(w_out, k)
-            xp = lax.ppermute(res[own + k][0], 'dp', swap)
-            dhp = lax.ppermute(res[own + k][1], 'dp', swap)
-            pre_p = mm(xp, w1, ((1,), (0,))).astype(BF16)
-            act_p = jnp.maximum(pre_p, 0)
-            da_p = jnp.where(pre_p > 0, mm(dhp, w2, ((1,), (1,))), 0.0).astype(BF16)
-            xq, dhq, act, da = res[k]
-            d_out = mm(act, dhq, ((0,), (0,))) + mm(act_p, dhp, ((0,), (0,)))
-            d_in = mm(xq, da, ((0,), (0,))) + mm(xp, da_p, ((0,), (0,)))
-            no, ro, co = optimizer_step(w2, d_out, weight(row_out, k), weight(col_out, k))
-            ni, ri, ci = optimizer_step(w1, d_in, weight(row_in, k), weight(col_in, k))
-            new_out.append(no.astype(BF16))
-            new_in.append(ni.astype(BF16))
-            stats.append((ri, ci, ro, co))
-
-        def assemble(mine, like):
-            theirs = [lax.ppermute(m, 'dp', swap) for m in mine]
-            out = jnp.zeros((el,) + mine[0].shape, like)
-            for k, m in enumerate(mine):
-                out = lax.dynamic_update_index_in_dim(out, m, lax.rem(base + k, el), 0)
-            for k, m in enumerate(theirs):
-                out = lax.dynamic_update_index_in_dim(out, m, lax.rem(base + own + k, el), 0)
-            return out
-
-        out_w_out = assemble(new_out, BF16)
-        out_w_in = assemble(new_in, BF16)
+            out_w_in = lax.dynamic_update_index_in_dim(out_w_in, new_in[k], place(own + k), 0)
+            out_w_out = lax.dynamic_update_index_in_dim(out_w_out, new_out[k], place(own + k), 0)
+        sizes = [s.shape[0] for s in stats[0]]
+        mine = jnp.stack([jnp.concatenate(s) for s in stats])
+        both = jnp.concatenate([mine, lax.ppermute(mine, 'dp', swap)], axis=0)
+        both = jnp.roll(both, base, axis=0)
         out_stats = []
-        for i in range(4):
-            mine = jnp.stack([s[i] for s in stats])
-            both = jnp.concatenate([mine, lax.ppermute(mine, 'dp', swap)], axis=0)
-            out_stats.append(jnp.roll(both, base, axis=0))
+        at = 0
+        for size in sizes:
+            out_stats.append(both[:, at:at + size])
+            at += size
 
         g_buf = jnp.stack([g_pos[q].reshape(ep_size, cap) for q in range(el)], axis=1)
         g_back = lax.all_to_all(g_buf, 'ep', 0, 0, tiled=True)

time: 1620 us -> 1530 us (0.944)
  matrix products: 560 us -> 40.7 us
  Pallas kernels: 0 us -> 500 us
  other arithmetic: 188 us -> 76.4 us
  waiting for transfers between devices: 454 us -> 539 us
  local copies, waits for them, and re-layouts: 248 us -> 222 us
    dot_general x30 -> x6, matrix products: 560 us -> 40.7 us  [mm(): return lax.dot_general(a, b, (dims, ((), ())), preferred_element_type=F32)]
    pallas_call x0 -> x4, Pallas kernels: none -> 500 us  [expert_call(): pl.pallas_call(functools.partial(expert_kernel, opt, nb), grid_spec=pltpu...]
    ppermute x4 -> x1, waiting for transfers between devices: 360 us -> 0.01 us  [local_step(): both = jnp.concatenate([mine, lax.ppermute(mine, 'dp', swap)], axis=0)]
    ppermute x8 -> x9, waiting for transfers between devices: 0.02 us -> 281 us  [the longest x2 106 us: local_step(): yp[q - own] = lax.ppermute(ys[q], 'dp', swap)]
    all_to_all x4, waiting for transfers between devices: 44.1 us -> 125 us  [local_step(): lax.all_to_all(dbuf.reshape(ep_size, cap, width), 'ep', 0, 0, tiled=True)]
    psum x1, waiting for transfers between devices: 0.01 us -> 68.9 us  [local_step(): lax.psum(gr[:, :experts] + (gr[:, experts:2 * experts] + gr[:, 2 * expert...]
    convert_element_type x8 -> x0, other arithmetic: 40.5 us -> none  [local_step(): dhq = (pq[:, None] * yq).astype(BF16)]
    dynamic_update_slice x4 -> x0, other arithmetic: 33.4 us -> none  [assemble(): out = lax.dynamic_update_index_in_dim(out, m, lax.rem(base + k, el), 0)]
  transfers between devices with their start and end apart: 26 -> 24, of which waited for: 12 -> 11; matrix products, arithmetic and copies ran while one was open for 49% -> 20% of each run, Pallas kernels for 0% -> 21%
where the time goes in v2:
time: 1530 us; the launch traced here: 1520 us
  waiting for transfers between devices  539 us (35%)
  Pallas kernels  500 us (33%)
  local copies, waits for them, and re-layouts  222 us (15%)
  other arithmetic  76.4 us (5%)
  starting transfers between devices  71.6 us (5%)
  blocking collectives  50.4 us (3%)
  matrix products  40.7 us (3%)
  between operations  17.2 us (1%)
    pallas_call x4, Pallas kernels, expert_call(): pl.pallas_call(functools.partial(expert_kernel, opt, nb), grid_spec=pltpu...  500 us
    gather x8, local copies, waits for them, and re-layouts, send(): jnp.take(rows, src_pos[:, q].reshape(-1), axis=0, mode='fill', fill_value=0)  132 us
    all_to_all x4, waiting for transfers between devices, local_step(): lax.all_to_all(dbuf.reshape(ep_size, cap, width), 'ep', 0, 0, tiled=True)  125 us
    ppermute x2, waiting for transfers between devices, local_step(): yp[q - own] = lax.ppermute(ys[q], 'dp', swap)  106 us
    ppermute x2, waiting for transfers between devices, local_step(): new_out.append(lax.ppermute(no, 'dp', swap))  90.9 us
    ppermute x2, waiting for transfers between devices, local_step(): xp[q - own] = lax.ppermute(xs[q], 'dp', swap)  83.5 us
    psum x1, waiting for transfers between devices, local_step(): lax.psum(gr[:, :experts] + (gr[:, experts:2 * experts] + gr[:, 2 * expert...  68.9 us
    all_to_all x7, waiting for transfers between devices, send(): lax.all_to_all(buf, 'ep', 0, 0, tiled=True).reshape(ep_size * cap, width)  60.3 us
  transfers between devices with their start and end apart: 24, of which 11 were waited for; matrix products, arithmetic and copies ran while one was open for 20% of the time, Pallas kernels for 21%

profile of v2, /device:TPU:0, one launch (start us, length us, event | category | flops | bytes accessed | tf_op | source)
XLA Modules:
  0.0 1516.6 jit_solution(9940667493561974634)
XLA Ops:
  48.0 16.5 %gather_fusion.1 = bf16[2560,768]{1,0:T(8,128)(2,1)} fusion(bf16[8192,768]{1,0:T(8,128)(2,1)} %param.17, s32[3072]{0:T(1024)S(1)} %pad_clamp_fusion.3), kind=kCustom, calls=%fused_computation.clone | custom fusion | bytes 7874560 | tf_op jit(solution)/shard_map/jit(_take)/gather | solution.py:301
  64.5 16.5 %gather_fusion.2 = bf16[2560,768]{1,0:T(8,128)(2,1)} fusion(bf16[8192,768]{1,0:T(8,128)(2,1)} %param.20, s32[3072]{0:T(1024)S(1)} %pad_clamp_fusion.3), kind=kCustom, calls=%fused_computation.1.clone | custom fusion | bytes 7874560 | tf_op jit(solution)/shard_map/jit(_take)/gather | solution.py:301
  91.8 16.5 %gather_fusion.4 = bf16[2560,768]{1,0:T(8,128)(2,1)} fusion(bf16[8192,768]{1,0:T(8,128)(2,1)} %param.20, s32[3072]{0:T(1024)S(1)} %pad_clamp_fusion.2), kind=kCustom, calls=%fused_computation.3.clone | custom fusion | bytes 7874560 | tf_op jit(solution)/shard_map/jit(_take)/gather | solution.py:301
  108.3 16.5 %gather_fusion.3 = bf16[2560,768]{1,0:T(8,128)(2,1)} fusion(bf16[8192,768]{1,0:T(8,128)(2,1)} %param.17, s32[3072]{0:T(1024)S(1)} %pad_clamp_fusion.2), kind=kCustom, calls=%fused_computation.2.clone | custom fusion | bytes 7874560 | tf_op jit(solution)/shard_map/jit(_take)/gather | solution.py:301
  137.9 50.4 %all_to_all.70 = bf16[8,320,768]{2,1,0:T(8,128)(2,1)} all-to-all(bf16[8,320,768]{2,1,0:T(8,128)(2,1)} %bitcast.68), channel_id=1, replica_groups=mesh['dp'=2,'ep'=8] {'ep'}, dimensions={0} | all-to-all | bytes 7864320 | tf_op jit(solution)/shard_map/all_to_all | solution.py:303
  193.3 16.5 %gather_fusion.8 = bf16[2560,768]{1,0:T(8,128)(2,1)} fusion(bf16[8192,768]{1,0:T(8,128)(2,1)} %param.20, s32[3072]{0:T(1024)S(1)} %pad_clamp_fusion), kind=kCustom, calls=%fused_computation.7.clone | custom fusion | bytes 7874560 | tf_op jit(solution)/shard_map/jit(_take)/gather | solution.py:301
  209.8 16.5 %gather_fusion.7 = bf16[2560,768]{1,0:T(8,128)(2,1)} fusion(bf16[8192,768]{1,0:T(8,128)(2,1)} %param.17, s32[3072]{0:T(1024)S(1)} %pad_clamp_fusion), kind=kCustom, calls=%fused_computation.6.clone | custom fusion | bytes 7874560 | tf_op jit(solution)/shard_map/jit(_take)/gather | solution.py:301
  244.0 46.1 %all-to-all-done.7 = bf16[8,320,768]{2,1,0:T(8,128)(2,1)} async-done(((bf16[8,320,768]{2,1,0:T(8,128)(2,1)}), bf16[8,320,768]{2,1,0:T(8,128)(2,1)}, u32[]{:S(2)}, u32[]{:S(2)}) %all-to-all-start.7) | async-done | bytes 3932192 | tf_op jit(solution)/shard_map/all_to_all | solution.py:303
  295.1 16.5 %gather_fusion.6 = bf16[2560,768]{1,0:T(8,128)(2,1)} fusion(bf16[8192,768]{1,0:T(8,128)(2,1)} %param.20, s32[3072]{0:T(1024)S(1)} %pad_clamp_fusion.1), kind=kCustom, calls=%fused_computation.5.clone | custom fusion | bytes 7874560 | tf_op jit(solution)/shard_map/jit(_take)/gather | solution.py:301
  311.6 16.6 %gather_fusion.5 = bf16[2560,768]{1,0:T(8,128)(2,1)} fusion(bf16[8192,768]{1,0:T(8,128)(2,1)} %param.17, s32[3072]{0:T(1024)S(1)} %pad_clamp_fusion.1), kind=kCustom, calls=%fused_computation.4.clone | custom fusion | bytes 7874560 | tf_op jit(solution)/shard_map/jit(_take)/gather | solution.py:301
  361.8 63.7 %expert_rows.3 = (bf16[2560,768]{1,0:T(8,128)(2,1)}, f32[2560,1]{1,0:T(8,128)}) custom-call(s32[1]{0:T(128)} %bitcast.31.ids, bf16[2560,768]{1,0:T(8,128)(2,1)} %bitcast.71, bf16[2560,768]{1,0:T(8,128)(2,1)} %bitcast.10.refs_1_, f32[2560,1]{1,0:T(8,128)} %squeeze.64.refs_2_, bf16[4,768,3072]{2,1,0:T(8,128)(2,1)} %refs_3_.3, bf16[4,3072,768]{2,1,0:T(8,128)(2,1)} %refs_4_.3), custom_call_target="tpu_custom_call" | custom-call | flops 48318382080 | bytes 25165824 | tf_op jit(solution)/shard_map/expert_rows/pallas_call | solution.py:214
  434.5 63.7 %expert_rows.2 = (bf16[2560,768]{1,0:T(8,128)(2,1)}, f32[2560,1]{1,0:T(8,128)}) custom-call(s32[1]{0:T(128)} %bitcast.30.ids, bf16[2560,768]{1,0:T(8,128)(2,1)} %bitcast.20.refs_0_, bf16[2560,768]{1,0:T(8,128)(2,1)} %bitcast.22.refs_1_, f32[2560,1]{1,0:T(8,128)} %squeeze.63.refs_2_, bf16[4,768,3072]{2,1,0:T(8,128)(2,1)} %refs_3_.3, bf16[4,3072,768]{2,1,0:T(8,128)(2,1)} %refs_4_.3), custom_call_target="tpu_custom_call" | custom-call | flops 48318382080 | bytes 25165824 | tf_op jit(solution)/shard_map/expert_rows/pallas_call | solution.py:214
  505.3 106.1 %collective-permute-done.4.refs_4_ = bf16[2560,768]{1,0:T(8,128)(2,1)} collective-permute-done((bf16[2560,768]{1,0:T(8,128)(2,1)}, bf16[2560,768]{1,0:T(8,128)(2,1)}, u32[]{:S(2)}, u32[]{:S(2)}) %collective-permute-start.4) | collective-permute-done | bytes 3932192 | tf_op jit(solution)/shard_map/ppermute | solution.py:318
  611.4 83.5 %collective-permute-done.3.refs_3_ = bf16[2560,768]{1,0:T(8,128)(2,1)} collective-permute-done((bf16[2560,768]{1,0:T(8,128)(2,1)}, bf16[2560,768]{1,0:T(8,128)(2,1)}, u32[]{:S(2)}, u32[]{:S(2)}) %collective-permute-start.3) | collective-permute-done | bytes 3932192 | tf_op jit(solution)/shard_map/ppermute | solution.py:315
  695.5 185.9 %expert_opt.2 = (bf16[2560,768]{1,0:T(8,128)(2,1)}, f32[2560,1]{1,0:T(8,128)}, bf16[768,3072]{1,0:T(8,128)(2,1)}, bf16[3072,768]{1,0:T(8,128)(2,1)}, bf16[4,768,...) custom-call(s32[1]{0:T(128)} %bitcast.14.ids, ...), custom_call_target="tpu_custom_call" | custom-call | flops 120795955200 | bytes 25165824 | tf_op jit(solution)/shard_map/expert_opt/pallas_call | solution.py:214
  881.4 186.3 %expert_opt.3 = (bf16[2560,768]{1,0:T(8,128)(2,1)}, f32[2560,1]{1,0:T(8,128)}, bf16[768,3072]{1,0:T(8,128)(2,1)}, bf16[3072,768]{1,0:T(8,128)(2,1)}, bf16[4,768,...) custom-call(s32[1]{0:T(128)} %bitcast.ids, ...), custom_call_target="tpu_custom_call", output_to_operand_aliasing={{4}: (13, {}), {5}: (14, {})} | custom-call | flops 120795955200 | bytes 25165824 | tf_op jit(solution)/shard_map/expert_opt/pallas_call | solution.py:214
  1089.8 40.4 %all-to-all-done.13 = bf16[8,320,768]{2,1,0:T(8,128)(2,1)} async-done(((bf16[8,320,768]{2,1,0:T(8,128)(2,1)}), bf16[8,320,768]{2,1,0:T(8,128)(2,1)}, u32[]{:S(2)}, u32[]{:S(2)}) %all-to-all-start.13) | async-done | bytes 3932192 | tf_op jit(solution)/shard_map/all_to_all | solution.py:337
  1140.0 41.6 %all-to-all-done.12 = bf16[8,320,768]{2,1,0:T(8,128)(2,1)} async-done(((bf16[8,320,768]{2,1,0:T(8,128)(2,1)}), bf16[8,320,768]{2,1,0:T(8,128)(2,1)}, u32[]{:S(2)}, u32[]{:S(2)}) %all-to-all-start.12) | async-done | bytes 3932192 | tf_op jit(solution)/shard_map/all_to_all | solution.py:337
  1189.0 43.3 %all-to-all-done.11 = bf16[8,320,768]{2,1,0:T(8,128)(2,1)} async-done(((bf16[8,320,768]{2,1,0:T(8,128)(2,1)}), bf16[8,320,768]{2,1,0:T(8,128)(2,1)}, u32[]{:S(2)}, u32[]{:S(2)}) %all-to-all-start.11) | async-done | bytes 3932192 | tf_op jit(solution)/shard_map/all_to_all | solution.py:337
  1247.4 68.9 %all-reduce.2.cloned.1.call-done = f32[768,32]{0,1:T(8,128)} async-done(((f32[768,32]{0,1:T(8,128)}), f32[768,32]{0,1:T(8,128)}) %all-reduce.2.cloned.1.call-update) | async-done | bytes 98320 | tf_op jit(solution)/shard_map/psum | solution.py:366
  1323.1 20.9 %pad_maximum_fusion = bf16[10240,768]{1,0:T(8,128)(2,1)} fusion(bf16[2560,768]{1,0:T(8,128)(2,1)} %bitcast.44, bf16[2560,768]{1,0:T(8,128)(2,1)} %bitcast.42, bf16[2560,768]{1,0:T(8,128)(2,1)} %bitcast.40, bf16[2560,768]{1,0:T(8,128)(2,1)} %bitcast.38), kind=kLoop, calls=%fused_computation.22 | loop fusion | flops 62914560 | bytes 31457280 | tf_op jit(solution)/shard_map/concatenate | solution.py:371
  1343.9 44.5 %gather_fusion = bf16[8192,768]{1,0:T(8,128)(2,1)} fusion(bf16[10240,768]{1,0:T(8,128)(2,1)} %pad_maximum_fusion, s32[8192]{0:T(1024)S(1)} %copy-done.19), kind=kCustom, calls=%fused_computation.8 | custom fusion | bytes 25198592 | tf_op jit(solution)/shard_map/jit(_take)/gather | solution.py:374
  1388.5 10.8 add_convert_fusion
  1404.2 90.9 %collective-permute-done.7 = bf16[3072,768]{1,0:T(8,128)(2,1)} collective-permute-done((bf16[3072,768]{1,0:T(8,128)(2,1)}, bf16[3072,768]{1,0:T(8,128)(2,1)}, u32[]{:S(2)}, u32[]{:S(2)}) %collective-permute-start.7) | collective-permute-done | bytes 4718624 | tf_op jit(solution)/shard_map/ppermute | solution.py:335
  (225 shorter events, 220.4 us)
Async XLA Ops:
  33.9 53.1 %all-to-all-start.2 = ((f32[8,4,320]{2,1,0:T(4,128)}), f32[8,4,320]{2,1,0:T(4,128)S(1)}, u32[]{:S(2)}, u32[]{:S(2)}) async-start(f32[8,4,320]{2,1,0:T(4,128)} %fusion.61), calls=%async_computation.2 | async-start | bytes 98304 | tf_op jit(solution)/shard_map/all_to_all | solution.py:296
  87.0 50.9 %all-to-all-start = ((bf16[8,320,768]{2,1,0:T(8,128)(2,1)}), bf16[8,320,768]{2,1,0:T(8,128)(2,1)}, u32[]{:S(2)}, u32[]{:S(2)}) async-start(bf16[8,320,768]{2,1,0:T(8,128)(2,1)} %bitcast.66), calls=%async_computation | async-start | bytes 7864320 | tf_op jit(solution)/shard_map/all_to_all | solution.py:303
  188.4 51.0 %all-to-all-start.4 = ((bf16[8,320,768]{2,1,0:T(8,128)(2,1)}), bf16[8,320,768]{2,1,0:T(8,128)(2,1)}, u32[]{:S(2)}, u32[]{:S(2)}) async-start(bf16[8,320,768]{2,1,0:T(8,128)(2,1)} %bitcast.65), calls=%async_computation.4 | async-start | bytes 7864320 | tf_op jit(solution)/shard_map/all_to_all | solution.py:303
  239.4 50.7 %all-to-all-start.7 = ((bf16[8,320,768]{2,1,0:T(8,128)(2,1)}), bf16[8,320,768]{2,1,0:T(8,128)(2,1)}, u32[]{:S(2)}, u32[]{:S(2)}) async-start(bf16[8,320,768]{2,1,0:T(8,128)(2,1)} %bitcast.67), calls=%async_computation.7 | async-start | bytes 7864320 | tf_op jit(solution)/shard_map/all_to_all | solution.py:303
  290.1 67.0 %all-to-all-start.8 = ((bf16[8,320,768]{2,1,0:T(8,128)(2,1)}), bf16[8,320,768]{2,1,0:T(8,128)(2,1)}, u32[]{:S(2)}, u32[]{:S(2)}) async-start(bf16[8,320,768]{2,1,0:T(8,128)(2,1)} %bitcast.62), calls=%async_computation.8 | async-start | bytes 7864320 | tf_op jit(solution)/shard_map/all_to_all | solution.py:303
  341.3 10.6 collective-permute-start.2
  355.1 526.3 %collective-permute-start.1 = (bf16[2560,768]{1,0:T(8,128)(2,1)}, bf16[2560,768]{1,0:T(8,128)(2,1)}, u32[]{:S(2)}, u32[]{:S(2)}) collective-permute-start(bf16[2560,768]{1,0:T(8,128)(2,1)} %bitcast.10.refs_1_), channel_id=1, source_target_pairs={{0,8},{8,0},{1,9},{9,1},{2,10},{10,2},{3,11},{11,3},{4,12},{12,4},... | collective-permute-start | bytes 11796488 | tf_op jit(solution)/shard_map/ppermute | solution.py:318
  355.5 525.9 %collective-permute-start = (bf16[2560,768]{1,0:T(8,128)(2,1)}, bf16[2560,768]{1,0:T(8,128)(2,1)}, u32[]{:S(2)}, u32[]{:S(2)}) collective-permute-start(bf16[2560,768]{1,0:T(8,128)(2,1)} %bitcast.70), channel_id=1, source_target_pairs={{0,8},{8,0},{1,9},{9,1},{2,10},{10,2},{3,11},{11,3},{4,12},{12,4},... | collective-permute-start | bytes 11796488 | tf_op jit(solution)/shard_map/ppermute | solution.py:315
  357.1 72.8 %all-to-all-start.5 = ((bf16[8,320,768]{2,1,0:T(8,128)(2,1)}), bf16[8,320,768]{2,1,0:T(8,128)(2,1)}, u32[]{:S(2)}, u32[]{:S(2)}) async-start(bf16[8,320,768]{2,1,0:T(8,128)(2,1)} %bitcast.64), calls=%async_computation.5 | async-start | bytes 7864320 | tf_op jit(solution)/shard_map/all_to_all | solution.py:303
  427.9 183.5 %collective-permute-start.4 = (bf16[2560,768]{1,0:T(8,128)(2,1)}, bf16[2560,768]{1,0:T(8,128)(2,1)}, u32[]{:S(2)}, u32[]{:S(2)}) collective-permute-start(bf16[2560,768]{1,0:T(8,128)(2,1)} %bitcast.22.refs_1_), channel_id=1, source_target_pairs={{0,8},{8,0},{1,9},{9,1},{2,10},{10,2},{3,11},{11,3},{4,12},{12,4},... | collective-permute-start | bytes 11796488 | tf_op jit(solution)/shard_map/ppermute | solution.py:318
  428.4 266.5 %collective-permute-start.3 = (bf16[2560,768]{1,0:T(8,128)(2,1)}, bf16[2560,768]{1,0:T(8,128)(2,1)}, u32[]{:S(2)}, u32[]{:S(2)}) collective-permute-start(bf16[2560,768]{1,0:T(8,128)(2,1)} %bitcast.20.refs_0_), channel_id=1, source_target_pairs={{0,8},{8,0},{1,9},{9,1},{2,10},{10,2},{3,11},{11,3},{4,12},{12,4},... | collective-permute-start | bytes 11796488 | tf_op jit(solution)/shard_map/ppermute | solution.py:315
  429.9 70.6 %all-to-all-start.6 = ((bf16[8,320,768]{2,1,0:T(8,128)(2,1)}), bf16[8,320,768]{2,1,0:T(8,128)(2,1)}, u32[]{:S(2)}, u32[]{:S(2)}) async-start(bf16[8,320,768]{2,1,0:T(8,128)(2,1)} %bitcast.63), calls=%async_computation.6 | async-start | bytes 7864320 | tf_op jit(solution)/shard_map/all_to_all | solution.py:303
  500.6 380.8 %all-to-all-start.1 = ((bf16[8,320,768]{2,1,0:T(8,128)(2,1)}), bf16[8,320,768]{2,1,0:T(8,128)(2,1)}, u32[]{:S(2)}, u32[]{:S(2)}) async-start(bf16[8,320,768]{2,1,0:T(8,128)(2,1)} %bitcast.61), calls=%async_computation.1 | async-start | bytes 7864320 | tf_op jit(solution)/shard_map/all_to_all | solution.py:303
  1070.7 8.6 all-to-all-start.9
  1079.4 50.9 %all-to-all-start.13 = ((bf16[8,320,768]{2,1,0:T(8,128)(2,1)}), bf16[8,320,768]{2,1,0:T(8,128)(2,1)}, u32[]{:S(2)}, u32[]{:S(2)}) async-start(bf16[8,320,768]{2,1,0:T(8,128)(2,1)} %bitcast.72), calls=%async_computation.13 | async-start | bytes 7864320 | tf_op jit(solution)/shard_map/all_to_all | solution.py:337
  1085.2 160.5 %collective-permute-start.9 = (f32[2,7680]{1,0:T(2,128)S(1)}, f32[2,7680]{1,0:T(2,128)S(1)}, u32[]{:S(2)}, u32[]{:S(2)}) collective-permute-start(f32[2,7680]{1,0:T(2,128)S(1)} %pad_maximum_fusion.1), channel_id=1, source_target_pairs={{0,8},{8,0},{1,9},{9,1},{2,10},{10,2},{3,11},{11,3},{4,12},{12,4},... | collective-permute-start | bytes 184328 | tf_op jit(solution)/shard_map/ppermute | solution.py:345
  1085.7 414.3 %collective-permute-start.6 = (bf16[768,3072]{1,0:T(8,128)(2,1)}, bf16[768,3072]{1,0:T(8,128)(2,1)}, u32[]{:S(2)}, u32[]{:S(2)}) collective-permute-start(bf16[768,3072]{1,0:T(8,128)(2,1)} %get-tuple-element.40), channel_id=1, source_target_pairs={{0,8},{8,0},{1,9},{9,1},{2,10},{10,2},{3,11},{11,3},{4,12},{12,4},... | collective-permute-start | bytes 14155784 | tf_op jit(solution)/shard_map/ppermute | solution.py:334
  1087.2 417.5 %collective-permute-start.8 = (bf16[3072,768]{1,0:T(8,128)(2,1)}, bf16[3072,768]{1,0:T(8,128)(2,1)}, u32[]{:S(2)}, u32[]{:S(2)}) collective-permute-start(bf16[3072,768]{1,0:T(8,128)(2,1)} %get-tuple-element.43), channel_id=1, source_target_pairs={{0,8},{8,0},{1,9},{9,1},{2,10},{10,2},{3,11},{11,3},{4,12},{12,4},... | collective-permute-start | bytes 14155784 | tf_op jit(solution)/shard_map/ppermute | solution.py:335
  1087.7 311.6 %collective-permute-start.5 = (bf16[768,3072]{1,0:T(8,128)(2,1)}, bf16[768,3072]{1,0:T(8,128)(2,1)}, u32[]{:S(2)}, u32[]{:S(2)}) collective-permute-start(bf16[768,3072]{1,0:T(8,128)(2,1)} %get-tuple-element.39), channel_id=1, source_target_pairs={{0,8},{8,0},{1,9},{9,1},{2,10},{10,2},{3,11},{11,3},{4,12},{12,4},... | collective-permute-start | bytes 14155784 | tf_op jit(solution)/shard_map/ppermute | solution.py:334
  1089.3 405.8 %collective-permute-start.7 = (bf16[3072,768]{1,0:T(8,128)(2,1)}, bf16[3072,768]{1,0:T(8,128)(2,1)}, u32[]{:S(2)}, u32[]{:S(2)}) collective-permute-start(bf16[3072,768]{1,0:T(8,128)(2,1)} %get-tuple-element.42), channel_id=1, source_target_pairs={{0,8},{8,0},{1,9},{9,1},{2,10},{10,2},{3,11},{11,3},{4,12},{12,4},... | collective-permute-start | bytes 14155784 | tf_op jit(solution)/shard_map/ppermute | solution.py:335
  1130.3 51.3 %all-to-all-start.12 = ((bf16[8,320,768]{2,1,0:T(8,128)(2,1)}), bf16[8,320,768]{2,1,0:T(8,128)(2,1)}, u32[]{:S(2)}, u32[]{:S(2)}) async-start(bf16[8,320,768]{2,1,0:T(8,128)(2,1)} %bitcast.73), calls=%async_computation.12 | async-start | bytes 7864320 | tf_op jit(solution)/shard_map/all_to_all | solution.py:337
  1181.6 50.7 %all-to-all-start.11 = ((bf16[8,320,768]{2,1,0:T(8,128)(2,1)}), bf16[8,320,768]{2,1,0:T(8,128)(2,1)}, u32[]{:S(2)}, u32[]{:S(2)}) async-start(bf16[8,320,768]{2,1,0:T(8,128)(2,1)} %bitcast.74), calls=%async_computation.11 | async-start | bytes 7864320 | tf_op jit(solution)/shard_map/all_to_all | solution.py:337
  1232.3 90.7 %all-to-all-start.10 = ((bf16[8,320,768]{2,1,0:T(8,128)(2,1)}), bf16[8,320,768]{2,1,0:T(8,128)(2,1)}, u32[]{:S(2)}, u32[]{:S(2)}) async-start(bf16[8,320,768]{2,1,0:T(8,128)(2,1)} %bitcast.69), calls=%async_computation.10 | async-start | bytes 7864320 | tf_op jit(solution)/shard_map/all_to_all | solution.py:337
  1236.9 79.4 %all-reduce.2.cloned.1.call-start = ((), (), s32[]{:S(2)}) async-start(), calls=%async_computation.14 | async-start | bytes 196608 | tf_op jit(solution)/shard_map/psum | solution.py:366
  (37 other events, 1476.5 us)
Sparse Core Ops, SparseCore 0:
  1245.8 70.4 all-reduce.1

commit v3 on v2

--- a/solution.py
+++ b/solution.py
@@ -8,14 +8,15 @@
 from jax.experimental.pallas import tpu as pltpu
 from jax.sharding import PartitionSpec as P
 
+
 OPT_STEP = 2
 DECAY_RATE = 1.0 - OPT_STEP ** -0.8
 LR_BASE = min(0.01, 1.0 / math.sqrt(OPT_STEP))
 AUX_COEF = 0.01
 F32 = jnp.float32
 BF16 = jnp.bfloat16
-ROW_BLOCK = 640
-F_CHUNK = 512
+OPT_TILE = (640, 1024, 3)
+ROWS_TILE = (640, 1536, 2)
 G_CHUNK = 64
 
 
@@ -47,16 +48,20 @@
     return sub_f, lane_f
 
 
-def expert_kernel(opt, own_blocks, ids, *refs):
+def expert_kernel(opt, has_back, own_blocks, ids, *refs):
+    if has_back:
+        at = 5
+        refs = refs[:at] + refs[at + 1:]
     if opt:
-        (x_own, y_own, p_own, x_par, y_par, p_par, w_in, w_out, sub_in, lane_in, sub_out, lane_out, full_in_i, full_out_i,
+        (x_ref, y_ref, p_ref, w_in, w_out, sub_in, lane_in, sub_out, lane_out, _, _,
          dbuf, g_out, new_in, new_out, full_in, full_out, sub_in_n, lane_in_n, sub_out_n, lane_out_n,
          w1, w2, sems, h_acc, b_acc, acc_in, acc_out, sub_f, lane_sum) = refs
     else:
-        (x_own, y_own, p_own, w_in, w_out, dbuf, g_out, w1, w2, sems, h_acc, b_acc) = refs
+        (x_ref, y_ref, p_ref, w_in, w_out, dbuf, g_out, w1, w2, sems, h_acc, b_acc) = refs
     step = pl.program_id(0)
     width, ff = w1.shape
-    chunks = ff // F_CHUNK
+    f_chunk = OPT_TILE[1] if opt else ROWS_TILE[1]
+    chunks = ff // f_chunk
 
     @pl.when(step == 0)
     def _():
@@ -70,10 +75,11 @@
             acc_in[...] = jnp.zeros_like(acc_in)
             acc_out[...] = jnp.zeros_like(acc_out)
 
-    def body(x_ref, y_ref, p_ref, own):
-        x = x_ref[...]
-        y = y_ref[...].astype(F32)
-        dh = (p_ref[...] * y).astype(BF16)
+    def body(own):
+        rows = p_ref.shape[0]
+        p = p_ref[...]
+        x = jnp.where(p > 0, x_ref[...].reshape(rows, width).astype(F32), 0.0).astype(BF16)
+        dh = (p * y_ref[...].reshape(rows, width).astype(F32)).astype(BF16)
         if opt:
             x_t = x.T
             dh_t = dh.T
@@ -81,9 +87,9 @@
             h_acc[...] = jnp.zeros_like(h_acc)
             b_acc[...] = jnp.zeros_like(b_acc)
 
-        @pl.loop(0, chunks)
+        @pl.loop(0, chunks, unroll=OPT_TILE[2] if opt else ROWS_TILE[2])
         def _(c):
-            at = pl.ds(pl.multiple_of(c * F_CHUNK, F_CHUNK), F_CHUNK)
+            at = pl.ds(pl.multiple_of(c * f_chunk, f_chunk), f_chunk)
             w1c = w1[:, at]
             w2c = w2[at, :]
             act = jnp.maximum(kdot(x, w1c, 1, 0).astype(BF16), 0)
@@ -98,17 +104,18 @@
 
         if own:
             h = h_acc[...].astype(BF16).astype(F32)
-            g_out[...] = jnp.sum(y_ref[...].astype(F32) * h, axis=1, keepdims=True)
-            dbuf[...] = b_acc[...].astype(BF16)
+            y = y_ref[...].reshape(rows, width).astype(F32)
+            g_out[...] = jnp.sum(y * h, axis=1, keepdims=True)
+            dbuf[...] = b_acc[...].astype(BF16).reshape(dbuf.shape)
 
     if opt:
         @pl.when(step < own_blocks)
         def _():
-            body(x_own, y_own, p_own, True)
+            body(True)
 
         @pl.when(step >= own_blocks)
         def _():
-            body(x_par, y_par, p_par, False)
+            body(False)
 
         @pl.when(step == pl.num_programs(0) - 1)
         def _():
@@ -120,6 +127,7 @@
                 def one(i, tot):
                     t = w[pl.ds(pl.multiple_of(i * G_CHUNK, G_CHUNK), G_CHUNK), :].astype(F32)
                     return tot + jnp.sum(jnp.sum(t * t, axis=1, keepdims=True), axis=0, keepdims=True)
+
                 tot = lax.fori_loop(0, rows // G_CHUNK, one, jnp.zeros((1, 1), F32))
                 return LR_BASE * jnp.maximum(1e-3, jnp.sqrt(tot * (1.0 / n)))
 
@@ -129,6 +137,7 @@
                     u = acc[at, :] * sub_f[at, :] * lane_f
                     acc[at, :] = u
                     return tot + jnp.sum(jnp.sum(u * u, axis=1, keepdims=True), axis=0, keepdims=True)
+
                 tot = lax.fori_loop(0, width // G_CHUNK, one, jnp.zeros((1, 1), F32))
                 return 1.0 / jnp.maximum(1.0, jnp.sqrt(tot * (1.0 / n)))
 
@@ -165,35 +174,40 @@
             o3.wait()
             o4.wait()
     else:
-        body(x_own, y_own, p_own, True)
-
-
-def expert_call(eid, x, y, p, w_in, w_out, partner=None, stats=None, full=None):
-    opt = partner is not None
-    rows, width = x.shape
-    el, _, ff = w_in.shape
-    nb = rows // ROW_BLOCK
-    steps = 2 * nb if opt else nb
-    own_map = lambda i, ids: (jnp.minimum(i, nb - 1), 0)
-    par_map = lambda i, ids: (jnp.maximum(i - nb, 0), 0)
+        body(True)
+
+
+def expert_call(ids, x, y, p, w_in, w_out, column, back=None, stats=None, full=None):
+    opt = stats is not None
+    groups, _, cap, _ = x[0].shape
+    el, width, ff = w_in.shape
+    row_block = OPT_TILE[0] if opt else ROWS_TILE[0]
+    per = row_block // cap
+    steps = groups // per
+    nb = steps // 2 if opt else steps
+    rows = nb * row_block
+    if opt:
+        at = lambda i, ids: jnp.where(i < nb, ids[1] * nb + i, (1 - ids[1]) * nb + i - nb)
+    else:
+        at = lambda i, ids: i
+    in_specs = [pl.BlockSpec((per, 1, cap, width), lambda i, ids, c=c, w=w: (at(i, ids), c, 0, w)) for _, c, w in (x, y)]
+    in_specs.append(pl.BlockSpec((row_block, 1), lambda i, ids: (at(i, ids), 0)))
+    args = [x[0], y[0], p]
+    out_map = lambda i, ids: (jnp.minimum(i, nb - 1), 0)
+    back_map = lambda i, ids: (jnp.minimum(i, nb - 1), column, 0, 0)
     fixed = lambda i, ids: (0, 0)
     any_spec = pl.BlockSpec(memory_space=pl.ANY)
-
-    def row_specs(m):
-        return [pl.BlockSpec((ROW_BLOCK, width), m), pl.BlockSpec((ROW_BLOCK, width), m), pl.BlockSpec((ROW_BLOCK, 1), m)]
-
-    in_specs = row_specs(own_map)
-    args = [x, y, p]
-    if opt:
-        in_specs += row_specs(par_map)
-        args += list(partner)
     in_specs += [any_spec, any_spec]
     args += [w_in, w_out]
-    out_shape = [jax.ShapeDtypeStruct((rows, width), BF16), jax.ShapeDtypeStruct((rows, 1), F32)]
-    out_specs = [pl.BlockSpec((ROW_BLOCK, width), own_map), pl.BlockSpec((ROW_BLOCK, 1), own_map)]
+    out_shape = [jax.ShapeDtypeStruct((rows // cap, el // 2, cap, width), BF16), jax.ShapeDtypeStruct((rows, 1), F32)]
+    out_specs = [pl.BlockSpec((per, 1, cap, width), back_map), pl.BlockSpec((row_block, 1), out_map)]
     scratch = [pltpu.VMEM((width, ff), BF16), pltpu.VMEM((ff, width), BF16), pltpu.SemaphoreType.DMA((4,)),
-               pltpu.VMEM((ROW_BLOCK, width), F32), pltpu.VMEM((ROW_BLOCK, width), F32)]
+               pltpu.VMEM((row_block, width), F32), pltpu.VMEM((row_block, width), F32)]
     aliases = {}
+    if back is not None:
+        aliases[1 + len(args)] = 0
+        in_specs.append(any_spec)
+        args.append(back)
     units = 4
     if opt:
         units = 10
@@ -204,7 +218,7 @@
         if full is None:
             full = (jnp.zeros((8, 128), BF16), jnp.zeros((8, 128), BF16))
         else:
-            aliases = {1 + len(args): 4, 2 + len(args): 5}
+            aliases.update({1 + len(args): 4, 2 + len(args): 5})
         args += list(full)
         s, l = jax.ShapeDtypeStruct((width, 1), F32), jax.ShapeDtypeStruct((1, ff), F32)
         out_shape += [jax.ShapeDtypeStruct((width, ff), BF16), jax.ShapeDtypeStruct((ff, width), BF16),
@@ -212,14 +226,35 @@
         out_specs += [any_spec] * 4 + [sub, lane, sub, lane]
         scratch += [pltpu.VMEM((width, ff), F32), pltpu.VMEM((width, ff), F32), pltpu.VMEM((width, 1), F32), pltpu.VMEM((8, ff), F32)]
     return pl.pallas_call(
-        functools.partial(expert_kernel, opt, nb),
+        functools.partial(expert_kernel, opt, back is not None, nb),
         grid_spec=pltpu.PrefetchScalarGridSpec(num_scalar_prefetch=1, grid=(steps,), in_specs=in_specs, out_specs=out_specs, scratch_shapes=scratch),
         out_shape=out_shape,
         input_output_aliases=aliases,
         compiler_params=pltpu.CompilerParams(dimension_semantics=('arbitrary',), vmem_limit_bytes=64_000_000),
         cost_estimate=pl.CostEstimate(flops=units * 2 * rows * width * ff, bytes_accessed=4 * rows * width * 2 + 4 * width * ff, transcendentals=0),
         name='expert_opt' if opt else 'expert_rows',
-    )(eid, *args)
+    )(ids, *args)
+
+
+def pair_kernel(x, y, _, out):
+    width = x.shape[1]
+    out[:, :width] = x[...]
+    out[:, width:] = y[...]
+
+
+def pair_rows(x, y, after):
+    rows, width = x.shape
+    tile = rows // 16
+    spec = pl.BlockSpec((tile, width), lambda i: (i, 0))
+    return pl.pallas_call(
+        pair_kernel,
+        grid=(16,),
+        in_specs=[spec, spec, pl.BlockSpec(memory_space=pl.ANY)],
+        out_specs=pl.BlockSpec((tile, 2 * width), lambda i: (i, 0)),
+        out_shape=jax.ShapeDtypeStruct((rows, 2 * width), x.dtype),
+        cost_estimate=pl.CostEstimate(flops=rows * width, bytes_accessed=8 * rows * width, transcendentals=0),
+        name='pair_rows',
+    )(x, y, after)
 
 
 def optimizer_step(weight, gradient, row_stat, col_stat):
@@ -257,7 +292,7 @@
     full_spec = P()
     swap = [(i, (i + 1) % dp_size) for i in range(dp_size)]
 
-    def local_step(x_tokens, expert_id, token_slot, grad_y, w_router, w_in, w_out, row_in, col_in, row_out, col_out, row_router, col_router):
+    def step_body(x_tokens, expert_id, token_slot, grad_y, w_router, w_in, w_out, row_in, col_in, row_out, col_out, row_router, col_router):
         tokens, width = x_tokens.shape
         el = w_in.shape[0]
         experts = w_router.shape[1]
@@ -277,14 +312,26 @@
             out = mm(onehot_b, cols, ((0,), (0,)))
             return [out[:, i * cap:(i + 1) * cap] for i in range(len(vals))]
 
-        t_hi, t_lo, t_cnt = to_slots([tok_idx // 64, tok_idx % 64, jnp.ones_like(tok_idx)])
-        src = (t_hi * 64.0 + t_lo).astype(jnp.int32)
-        src = jnp.where(t_cnt > 0.5, src, tokens)
-
-        def by_pos(table):
-            return jnp.roll(table.reshape(ep_size, el, cap), -base, axis=1)
-
-        src_pos = by_pos(src)
+        t_hi, t_lo = to_slots([tok_idx // 64, tok_idx % 64])
+        src = (t_hi * 64.0 + t_lo).astype(jnp.int32).reshape(ep_size, dp_size, own, cap)
+
+        def rows_of(table, index):
+            return jnp.take(table, index.reshape(-1), axis=0, mode='clip').reshape(index.shape + table.shape[1:])
+
+        def at_dp(table, i):
+            return lax.dynamic_index_in_dim(table, i, 1, keepdims=False)
+
+        def to_owners(table, k):
+            buf = rows_of(table, jnp.swapaxes(src[:, :, k], 0, 1))
+            buf = buf.reshape(dp_size * ep_size, 1, cap, -1)
+            return lax.all_to_all(buf, ('dp', 'ep'), 0, 0, tiled=True), buf
+
+        x_first, _ = to_owners(x_tokens, 0)
+        y_first, y_buf = to_owners(grad_y, 0)
+        xy_tok = pair_rows(x_tokens, grad_y, y_buf)
+        xy_own = [None] + [to_owners(xy_tok, k)[0] for k in range(1, own)]
+        buf = rows_of(xy_tok, at_dp(src, 1 - zi))
+        xy_non = lax.all_to_all(buf, 'ep', 0, 0, tiled=True)
 
         r_hi, r_mid, r_lo = split3(w_router)
         lg = mm(x_tokens, jnp.concatenate([r_hi, r_mid, r_lo], axis=1), ((1,), (0,)))
@@ -292,54 +339,42 @@
         gate_probs = jax.nn.softmax(logits, axis=-1)
         gate_val = jnp.sum(gate_probs * onehot, axis=-1)
         p_hi, p_mid, p_lo = to_slots(list(split3(gate_val)))
-        p_slot = p_hi + (p_mid + p_lo)
-        p_recv = lax.all_to_all(by_pos(p_slot), 'ep', 0, 0, tiled=True)
-        p_rows = jnp.swapaxes(p_recv, 0, 1).reshape(el, ep_size * cap, 1)
-        p_part = lax.ppermute(p_rows[own:].reshape(own, ep_size * cap), 'dp', swap).reshape(own, ep_size * cap, 1)
-
-        def send(rows, q):
-            buf = jnp.take(rows, src_pos[:, q].reshape(-1), axis=0, mode='fill', fill_value=0)
-            buf = buf.reshape(ep_size, cap, width)
-            return lax.all_to_all(buf, 'ep', 0, 0, tiled=True).reshape(ep_size * cap, width)
-
-        def place(q):
-            return lax.rem(base + q, el)
-
-        order = []
+        p_slot = (p_hi + (p_mid + p_lo)).reshape(ep_size, dp_size, own, cap)
+        p_all = jnp.broadcast_to(p_slot[None], (dp_size,) + p_slot.shape).reshape(dp_size * ep_size, dp_size, own, cap)
+        p_all = lax.all_to_all(p_all, ('dp', 'ep'), 0, 0, tiled=True)
+        p_own = lax.dynamic_index_in_dim(p_all, zi, 1, keepdims=False)
+        p_non = lax.dynamic_slice_in_dim(lax.dynamic_index_in_dim(p_all, 1 - zi, 1, keepdims=False), zi * ep_size, ep_size, 0)
+
+        def stat(table, e):
+            return lax.dynamic_index_in_dim(table, e, 0)
+
+        g_pos, new_in, new_out, stats = [], [], [], []
+        full = back_a = back_b = None
         for k in range(own):
-            order += [own + k, k]
-        xs, ys, xp, yp = {}, {}, {}, {}
-        for q in order:
-            xs[q] = send(x_tokens, q)
-            if q >= own:
-                xp[q - own] = lax.ppermute(xs[q], 'dp', swap)
-            ys[q] = send(grad_y, q)
-            if q >= own:
-                yp[q - own] = lax.ppermute(ys[q], 'dp', swap)
-
-        g_pos, back, new_in, new_out, stats = {}, {}, [], [], []
-        full = None
-        for q in order:
-            eid = place(q).reshape(1)
-            if q >= own:
-                dbuf, g_pos[q] = expert_call(eid, xs[q], ys[q], p_rows[q], w_in, w_out)
-            else:
-                st = (lax.dynamic_index_in_dim(row_in, place(q), 0, keepdims=False)[:, None],
-                      lax.dynamic_index_in_dim(col_in, place(q), 0),
-                      lax.dynamic_index_in_dim(col_out, place(q), 0, keepdims=False)[:, None],
-                      lax.dynamic_index_in_dim(row_out, place(q), 0))
-                dbuf, g_pos[q], ni, no, fi, fo, s_in, l_in, s_out, l_out = expert_call(
-                    eid, xs[q], ys[q], p_rows[q], w_in, w_out, (xp[q], yp[q], p_part[q]), st, full)
-                full = (fi, fo)
-                new_in.append(lax.ppermute(ni, 'dp', swap))
-                new_out.append(lax.ppermute(no, 'dp', swap))
-                stats.append((s_in[:, 0], l_in[0], l_out[0], s_out[:, 0]))
-            back[q] = lax.all_to_all(dbuf.reshape(ep_size, cap, width), 'ep', 0, 0, tiled=True).reshape(ep_size * cap, width)
+            e = base + k
+            ids = jnp.stack([e, zi])
+            st = (stat(row_in, e).reshape(width, 1), stat(col_in, e), stat(col_out, e).reshape(width, 1), stat(row_out, e))
+            back_b, g, ni, no, fi, fo, s_in, l_in, s_out, l_out = expert_call(ids, *(((xy_own[k], 0, 0), (xy_own[k], 0, 1)) if k else ((x_first, 0, 0), (y_first, 0, 0))), p_own[:, k].reshape(-1, 1), w_in, w_out, k, back=back_b, stats=st, full=full)
+            full = (fi, fo)
+            new_in.append(lax.ppermute(ni, 'dp', swap))
+            new_out.append(lax.ppermute(no, 'dp', swap))
+            stats.append((s_in[:, 0], l_in[0], l_out[0], s_out[:, 0]))
+            g_pos.append(g)
+        last = stats[-1][0]
+        for k in range(own):
+            e = lax.rem(base + own + k, el)
+            ids, _ = lax.optimization_barrier((jnp.stack([e, zi]), last))
+            back_a, g = expert_call(ids, (xy_non, k, 0), (xy_non, k, 1), p_non[:, k].reshape(-1, 1), w_in, w_out, k, back=back_a)
+            last = g
+            g_pos.append(g)
+        back_b = lax.all_to_all(back_b, 'ep', 0, 0, tiled=True)
+        back_a = lax.all_to_all(back_a, 'ep', 0, 0, tiled=True)
 
         out_w_in, out_w_out = full
         for k in range(own):
-            out_w_in = lax.dynamic_update_index_in_dim(out_w_in, new_in[k], place(own + k), 0)
-            out_w_out = lax.dynamic_update_index_in_dim(out_w_out, new_out[k], place(own + k), 0)
+            e = lax.rem(base + own + k, el)
+            out_w_in = lax.dynamic_update_index_in_dim(out_w_in, new_in[k], e, 0)
+            out_w_out = lax.dynamic_update_index_in_dim(out_w_out, new_out[k], e, 0)
         sizes = [s.shape[0] for s in stats[0]]
         mine = jnp.stack([jnp.concatenate(s) for s in stats])
         both = jnp.concatenate([mine, lax.ppermute(mine, 'dp', swap)], axis=0)
@@ -350,7 +385,7 @@
             out_stats.append(both[:, at:at + size])
             at += size
 
-        g_buf = jnp.stack([g_pos[q].reshape(ep_size, cap) for q in range(el)], axis=1)
+        g_buf = jnp.stack([g.reshape(ep_size, cap) for g in g_pos], axis=1)
         g_back = lax.all_to_all(g_buf, 'ep', 0, 0, tiled=True)
         g_slot = jnp.roll(g_back, base, axis=1).reshape(experts, cap)
         g3 = jnp.concatenate(split3(g_slot), axis=0)
@@ -368,14 +403,21 @@
         wcat = jnp.concatenate([r_hi, r_mid, r_hi, r_lo, r_mid, r_hi], axis=1)
         dx_router = mm(lcat, wcat, ((1,), (1,)))
 
-        back_all = jnp.concatenate([back[q] for q in range(el)], axis=0)
-        pos_e = lax.rem(expert_id % el - base + el, el)
-        back_pos = jnp.where(token_slot >= 0, (pos_e * ep_size + expert_id // el) * cap + token_slot, experts * cap)
-        dx_expert = jnp.take(back_all, back_pos, axis=0, mode='fill', fill_value=0)
+        slot_at = (expert_id // el * own + expert_id % own) * cap + token_slot
+        mine_e = expert_id % el // own == zi
+        nowhere = ep_size * own * cap
+
+        def rows_back(table, here):
+            index = jnp.where((token_slot >= 0) & here, slot_at, nowhere)
+            return jnp.take(table.reshape(nowhere, width), index, axis=0, mode='fill', fill_value=0)
+
+        dx_b = rows_back(back_b, mine_e)
+        dx_a = rows_back(back_a, jnp.logical_not(mine_e))
+        dx_expert = dx_b + dx_a
         grad_x = (dx_expert.astype(F32) + dx_router).astype(BF16)
         new_router, row_router_new, col_router_new = optimizer_step(w_router, grad_router, row_router, col_router)
         return (out_w_in, out_w_out, new_router, out_stats[0], out_stats[1], out_stats[2], out_stats[3], row_router_new, col_router_new, grad_x)
 
     in_specs = (row_spec, tok_spec, tok_spec, row_spec, full_spec, exp_spec, exp_spec, exp_spec, exp_spec, exp_spec, exp_spec, full_spec, full_spec)
     out_specs = (exp_spec, exp_spec, full_spec, exp_spec, exp_spec, exp_spec, exp_spec, full_spec, full_spec, row_spec)
-    return jax.shard_map(local_step, mesh=mesh, in_specs=in_specs, out_specs=out_specs, check_vma=False)
+    return jax.shard_map(step_body, mesh=mesh, in_specs=in_specs, out_specs=out_specs, check_vma=False)

time: 1530 us -> 1350 us (0.88)
  waiting for transfers between devices: 539 us -> 395 us
  local copies, waits for them, and re-layouts: 222 us -> 274 us
  blocking collectives: 50.4 us -> 0 us
  other arithmetic: 76.4 us -> 40.2 us
  Pallas kernels: 500 us -> 530 us
  starting transfers between devices: 71.6 us -> 43.8 us
    ppermute x10 -> x5, waiting for transfers between devices: 281 us -> 0.01 us  [the longest x2 0.01 us: step_body(): new_out.append(lax.ppermute(no, 'dp', swap))]
    all_to_all x13 -> x8, waiting for transfers between devices: 190 us -> 293 us  [the longest x3 216 us: to_owners(): return (lax.all_to_all(buf, ('dp', 'ep'), 0, 0, tiled=True), buf)]
    gather x9 -> x6, local copies, waits for them, and re-layouts: 177 us -> 228 us  [the longest x4 145 us: rows_of(): jnp.take(table, index.reshape(-1), axis=0, mode='clip')]
    all_to_all x1 -> x0, blocking collectives: 50.4 us -> none  [send(): lax.all_to_all(buf, 'ep', 0, 0, tiled=True).reshape(ep_size * cap, width)]
    psum x1, waiting for transfers between devices: 68.9 us -> 102 us  [step_body(): lax.psum(gr[:, :experts] + (gr[:, experts:2 * experts] + gr[:, 2 * expert...]
    pallas_call x4 -> x5, Pallas kernels: 500 us -> 530 us  [the longest x4 508 us: expert_call(): pl.pallas_call(functools.partial(expert_kernel, opt, back is not None, nb...]
    select_n x9 -> x0, other arithmetic: 24.2 us -> none  [the longest x8 24.2 us: send(): jnp.take(rows, src_pos[:, q].reshape(-1), axis=0, mode='fill', fill_value=0)]
    all_to_all x13 -> x8, starting transfers between devices: 61.4 us -> 38.3 us  [the longest x3 13.1 us: to_owners(): return (lax.all_to_all(buf, ('dp', 'ep'), 0, 0, tiled=True), buf)]
  transfers between devices with their start and end apart: 24 -> 14, of which waited for: 11 -> 6; matrix products, arithmetic and copies ran while one was open for 20% -> 20% of each run, Pallas kernels for 21% -> 39%
where the time goes in v3:
time: 1350 us; the launch traced here: 1340 us
  Pallas kernels  530 us (39%)
  waiting for transfers between devices  395 us (29%)
  local copies, waits for them, and re-layouts  274 us (20%)
  starting transfers between devices  43.8 us (3%)
  matrix products  42.7 us (3%)
  other arithmetic  40.2 us (3%)
  between operations  17.3 us (1%)
    pallas_call x4, Pallas kernels, expert_call(): pl.pallas_call(functools.partial(expert_kernel, opt, back is not None, nb...  508 us
    all_to_all x3, waiting for transfers between devices, to_owners(): return (lax.all_to_all(buf, ('dp', 'ep'), 0, 0, tiled=True), buf)  216 us
    gather x4, local copies, waits for them, and re-layouts, rows_of(): jnp.take(table, index.reshape(-1), axis=0, mode='clip')  145 us
    psum x1, waiting for transfers between devices, step_body(): lax.psum(gr[:, :experts] + (gr[:, experts:2 * experts] + gr[:, 2 * expert...  102 us
    gather x2, local copies, waits for them, and re-layouts, rows_back(): jnp.take(table.reshape(nowhere, width), index, axis=0, mode='fill', fill_...  82.7 us
    all_to_all x1, waiting for transfers between devices, step_body(): back_b = lax.all_to_all(back_b, 'ep', 0, 0, tiled=True)  76.7 us
    dot_general x6, matrix products, mm(): return lax.dot_general(a, b, (dims, ((), ())), preferred_element_type=F32)  42.7 us
  transfers between devices with their start and end apart: 14, of which 6 were waited for; matrix products, arithmetic and copies ran while one was open for 20% of the time, Pallas kernels for 39%

profile of v3, /device:TPU:0, one launch (start us, length us, event | category | flops | bytes accessed | tf_op | source)
XLA Modules:
  0.0 1344.0 jit_solution(4245651646446370694)
XLA Ops:
  10.7 8.5 convolution_bitcast_fusion
  21.4 6.2 fusion.12
  32.9 5.3 all-to-all-start.1
  38.1 5.8 fusion.6
  44.2 29.7 %gather_fusion.2 = bf16[5120,768]{1,0:T(8,128)(2,1)} fusion(bf16[8192,768]{1,0:T(8,128)(2,1)} %x.1, s32[5120]{0:T(1024)S(1)} %broadcast_clamp_fusion.4), kind=kCustom, calls=%fused_computation.4 | custom fusion | bytes 15749120 | tf_op jit(solution)/shard_map/jit(_take)/gather | solution.py:319
  78.0 29.7 %gather_fusion = bf16[5120,768]{1,0:T(8,128)(2,1)} fusion(bf16[8192,768]{1,0:T(8,128)(2,1)} %y.1, s32[5120]{0:T(1024)S(1)} %broadcast_clamp_fusion.4), kind=kCustom, calls=%fused_computation.2 | custom fusion | bytes 15749120 | tf_op jit(solution)/shard_map/jit(_take)/gather | solution.py:319
  107.8 65.6 %all-to-all-done.2.refs_0_ = bf16[16,1,320,768]{3,2,1,0:T(8,128)(2,1)} async-done(((bf16[16,1,320,768]{3,2,1,0:T(8,128)(2,1)}), bf16[16,1,320,768]{3,2,1,0:T(8,128)(2,1)}, u32[]{:S(2)}, u32[]{:S(2)}) %all-to-all-start.2) | async-done | bytes 7864352 | tf_op jit(solution)/shard_map/all_to_all | solution.py:327
  177.9 22.1 %pair_rows.1 = bf16[8192,1536]{1,0:T(8,128)(2,1)} custom-call(bf16[8192,768]{1,0:T(8,128)(2,1)} %x.1, bf16[8192,768]{1,0:T(8,128)(2,1)} %y.1, bf16[16,1,320,768]{3,2,1,0:T(8,128)(2,1)} %bitcast.65), custom_call_target="tpu_custom_call" | custom-call | flops 6291456 | bytes 50331648 | tf_op jit(solution)/shard_map/pair_rows/pallas_call | solution.py:249
  200.0 42.6 %gather_fusion.1 = bf16[5120,1536]{1,0:T(8,128)(2,1)} fusion(bf16[8192,1536]{1,0:T(8,128)(2,1)} %pair_rows.1, s32[5120]{0:T(1024)S(1)} %broadcast_clamp_fusion.3), kind=kCustom, calls=%fused_computation.3 | custom fusion | bytes 31477760 | tf_op jit(solution)/shard_map/jit(_take)/gather | solution.py:319
  242.6 30.7 %all-to-all-done.3.refs_1_ = bf16[16,1,320,768]{3,2,1,0:T(8,128)(2,1)} async-done(((bf16[16,1,320,768]{3,2,1,0:T(8,128)(2,1)}), bf16[16,1,320,768]{3,2,1,0:T(8,128)(2,1)}, u32[]{:S(2)}, u32[]{:S(2)}) %all-to-all-start.3) | async-done | bytes 7864352 | tf_op jit(solution)/shard_map/all_to_all | solution.py:327
  283.4 42.7 %gather_fusion.3 = bf16[5120,1536]{1,0:T(8,128)(2,1)} fusion(bf16[8192,1536]{1,0:T(8,128)(2,1)} %pair_rows.1, s32[5120]{0:T(1024)S(1)} %broadcast_clamp_fusion.2), kind=kCustom, calls=%fused_computation.5 | custom fusion | bytes 31477760 | tf_op jit(solution)/shard_map/jit(_take)/gather | solution.py:319
  346.4 119.6 %all-to-all-done.refs_0_.refs_1_ = bf16[16,1,320,1536]{3,2,1,0:T(8,128)(2,1)} async-done(((bf16[16,1,320,1536]{3,2,1,0:T(8,128)(2,1)}), bf16[16,1,320,1536]{3,2,1,0:T(8,128)(2,1)}, u32[]{:S(2)}, u32[]{:S(2)}) %all-to-all-start) | async-done | bytes 15728672 | tf_op jit(solution)/shard_map/all_to_all | solution.py:327
  466.0 5.7 all-to-all-start.4
  472.2 192.9 %expert_opt.2 = (bf16[8,2,320,768]{3,2,1,0:T(8,128)(2,1)}, f32[2560,1]{1,0:T(8,128)}, bf16[768,3072]{1,0:T(8,128)(2,1)}, bf16[3072,768]{1,0:T(8,128)(2,1)}, bf16...) custom-call(s32[2]{0:T(128)} %pad_add_fusion.1.ids, ...), custom_call_target="tpu_custom_call" | custom-call | flops 120795955200 | bytes 25165824 | tf_op jit(solution)/shard_map/expert_opt/pallas_call | solution.py:228
  672.7 200.5 %expert_opt.3 = (bf16[8,2,320,768]{3,2,1,0:T(8,128)(2,1)}, f32[2560,1]{1,0:T(8,128)}, bf16[768,3072]{1,0:T(8,128)(2,1)}, bf16[3072,768]{1,0:T(8,128)(2,1)}, bf16...) custom-call(s32[2]{0:T(128)} %pad_add_fusion.ids, ...), custom_call_target="tpu_custom_call", output_to_operand_aliasing={{0}: (6, {}), {4}: (11, {}), {5}: (12, {})} | custom-call | flops 120795955200 | bytes 25165824 | tf_op jit(solution)/shard_map/expert_opt/pallas_call | solution.py:228
  881.5 57.3 %expert_rows.2 = (bf16[8,2,320,768]{3,2,1,0:T(8,128)(2,1)}, f32[2560,1]{1,0:T(8,128)}) custom-call(s32[2]{0:T(128)} %pad_add_fusion.2.ids, bf16[8,2,320,1536]{3,2,1,0:T(8,128)(2,1)} %all-to-all-done.4.refs_0_.refs_1_, bf16[8,2,320,1536]{3,2,1,0:T(8,128)(2,1)} %all-to-all-done.4.refs_0_.refs_1_, f32[2560,1]{1,0:T(8,128)} %reshape_squeeze.18.refs_2_, ...), custom_call_target="tpu_custom_call" | custom-call | flops 48318382080 | bytes 25165824 | tf_op jit(solution)/shard_map/expert_rows/pallas_call | solution.py:228
  940.6 57.7 %expert_rows.3 = (bf16[8,2,320,768]{3,2,1,0:T(8,128)(2,1)}, f32[2560,1]{1,0:T(8,128)}) custom-call(s32[2]{0:T(128)} %pad_add_fusion.3.ids, bf16[8,2,320,1536]{3,2,1,0:T(8,128)(2,1)} %all-to-all-done.4.refs_0_.refs_1_, bf16[8,2,320,1536]{3,2,1,0:T(8,128)(2,1)} %all-to-all-done.4.refs_0_.refs_1_, ...), custom_call_target="tpu_custom_call", output_to_operand_aliasing={{0}: (6, {})} | custom-call | flops 48318382080 | bytes 25165824 | tf_op jit(solution)/shard_map/expert_rows/pallas_call | solution.py:228
  1010.0 5.2 all-to-all-start.6
  1026.9 76.7 %all-to-all-done.6 = bf16[8,2,320,768]{3,2,1,0:T(8,128)(2,1)} async-done(((bf16[8,2,320,768]{3,2,1,0:T(8,128)(2,1)}), bf16[8,2,320,768]{3,2,1,0:T(8,128)(2,1)}, u32[]{:S(2)}, u32[]{:S(2)}) %all-to-all-start.6) | async-done | bytes 7864352 | tf_op jit(solution)/shard_map/all_to_all | solution.py:370
  1110.7 6.7 fusion.29
  1119.9 102.5 %all-reduce.2.cloned.1.call-done = f32[768,32]{0,1:T(8,128)} async-done(((f32[768,32]{0,1:T(8,128)}), f32[768,32]{0,1:T(8,128)}) %all-reduce.2.cloned.1.call-update) | async-done | bytes 98320 | tf_op jit(solution)/shard_map/psum | solution.py:401
  1238.8 41.3 %gather_fusion.4 = bf16[8192,768]{1,0:T(8,128)(2,1)} fusion(bf16[5120,768]{1,0:T(8,128)(2,1)} %bitcast.30, s32[8192]{0:T(1024)S(1)} %copy-done.20), kind=kCustom, calls=%fused_computation.clone | custom fusion | bytes 25198592 | tf_op jit(solution)/shard_map/jit(_take)/gather | solution.py:412
  1280.2 41.3 %gather_fusion.5 = bf16[8192,768]{1,0:T(8,128)(2,1)} fusion(bf16[5120,768]{1,0:T(8,128)(2,1)} %bitcast.31, s32[8192]{0:T(1024)S(1)} %copy-done.19), kind=kCustom, calls=%fused_computation.1.clone | custom fusion | bytes 25198592 | tf_op jit(solution)/shard_map/jit(_take)/gather | solution.py:412
  1321.5 15.2 %add_convert_fusion = bf16[8192,768]{1,0:T(8,128)(2,1)} fusion(bf16[8192,192]{0,1:T(8,128)(2,1)} %get-tuple-element.77, bf16[768,192]{0,1:T(8,128)(2,1)S(1)} %copy-done.28, bf16[8192,768]{1,0:T(8,128)(2,1)} %gather_fusion.5, bf16[8192,768]{1,0:T(8,128)(2,1)} %gather_fusion.4, pred[8192]{0:T(1024)(128)(4,1)S(1)} %copy-done.26, pred[8192]{0:T(1024)(128)(4,1)S(1)} %copy-done.29), kind=kOutput, calls=%fused_computation.6 | convolution fusion | flops 2453667840 | bytes 41205760 | tf_op jit(solution)/shard_map/dot_general | solution.py:283
  (189 shorter events, 115.2 us)
Async XLA Ops:
  32.9 41.1 %all-to-all-start.1 = ((f32[16,2,2,320]{3,2,1,0:T(2,128)}), f32[16,2,2,320]{3,2,1,0:T(2,128)S(1)}, u32[]{:S(2)}, u32[]{:S(2)}) async-start(f32[16,2,2,320]{3,2,1,0:T(2,128)} %bitcast.9), calls=%async_computation.1 | async-start | bytes 196608 | tf_op jit(solution)/shard_map/all_to_all | solution.py:344
  73.9 99.5 %all-to-all-start.2 = ((bf16[16,1,320,768]{3,2,1,0:T(8,128)(2,1)}), bf16[16,1,320,768]{3,2,1,0:T(8,128)(2,1)}, u32[]{:S(2)}, u32[]{:S(2)}) async-start(bf16[16,1,320,768]{3,2,1,0:T(8,128)(2,1)} %bitcast.68), calls=%async_computation.2 | async-start | bytes 15728640 | tf_op jit(solution)/shard_map/all_to_all | solution.py:327
  173.4 99.9 %all-to-all-start.3 = ((bf16[16,1,320,768]{3,2,1,0:T(8,128)(2,1)}), bf16[16,1,320,768]{3,2,1,0:T(8,128)(2,1)}, u32[]{:S(2)}, u32[]{:S(2)}) async-start(bf16[16,1,320,768]{3,2,1,0:T(8,128)(2,1)} %bitcast.64), calls=%async_computation.3 | async-start | bytes 15728640 | tf_op jit(solution)/shard_map/all_to_all | solution.py:327
  273.3 192.7 %all-to-all-start = ((bf16[16,1,320,1536]{3,2,1,0:T(8,128)(2,1)}), bf16[16,1,320,1536]{3,2,1,0:T(8,128)(2,1)}, u32[]{:S(2)}, u32[]{:S(2)}) async-start(bf16[16,1,320,1536]{3,2,1,0:T(8,128)(2,1)} %bitcast.66), calls=%async_computation | async-start | bytes 31457280 | tf_op jit(solution)/shard_map/all_to_all | solution.py:327
  283.4 45.8 %copy-start.12 = (bf16[768,32]{0,1:T(8,128)(2,1)S(1)}, bf16[768,32]{0,1:T(8,128)(2,1)}, u32[]{:S(2)}) copy-start(bf16[768,32]{0,1:T(8,128)(2,1)} %copy-done.11) | copy-start | bytes 147460
  283.4 46.4 %copy-start.33 = (f32[32]{0:T(128)S(1)}, f32[32]{0:T(128)}, u32[]{:S(2)}) copy-start(f32[32]{0:T(128)} %get-tuple-element.65) | copy-start | bytes 388
  283.4 47.0 %copy-start.7 = (s32[8192]{0:T(1024)S(1)}, s32[8192]{0:T(1024)}, u32[]{:S(2)}) copy-start(s32[8192]{0:T(1024)} %param.16) | copy-start | bytes 98308
  283.4 47.0 %copy-start.17 = (s32[8192]{0:T(1024)S(1)}, s32[8192]{0:T(1024)}, u32[]{:S(2)}) copy-start(s32[8192]{0:T(1024)} %param.17) | copy-start | bytes 98308
  283.4 48.9 %copy-start.23 = (f32[4,3072]{1,0:T(4,128)S(1)}, f32[4,3072]{1,0:T(4,128)}, u32[]{:S(2)}) copy-start(f32[4,3072]{1,0:T(4,128)} %param.24) | copy-start | bytes 147460
  283.4 48.9 %copy-start.24 = (f32[4,3072]{1,0:T(4,128)S(1)}, f32[4,3072]{1,0:T(4,128)}, u32[]{:S(2)}) copy-start(f32[4,3072]{1,0:T(4,128)} %param.23) | copy-start | bytes 147460
  466.0 415.5 %all-to-all-start.4 = ((bf16[8,2,320,1536]{3,2,1,0:T(8,128)(2,1)}), bf16[8,2,320,1536]{3,2,1,0:T(8,128)(2,1)}, u32[]{:S(2)}, u32[]{:S(2)}) async-start(bf16[8,2,320,1536]{3,2,1,0:T(8,128)(2,1)} %bitcast.67), calls=%async_computation.4 | async-start | bytes 31457280 | tf_op jit(solution)/shard_map/all_to_all | solution.py:334
  670.6 334.4 %collective-permute-start = (bf16[768,3072]{1,0:T(8,128)(2,1)}, bf16[768,3072]{1,0:T(8,128)(2,1)}, u32[]{:S(2)}, u32[]{:S(2)}) collective-permute-start(bf16[768,3072]{1,0:T(8,128)(2,1)} %get-tuple-element.41), channel_id=1, source_target_pairs={{0,8},{8,0},{1,9},{9,1},{2,10},{10,2},{3,11},{11,3},{4,12},{12,4},... | collective-permute-start | bytes 14155784 | tf_op jit(solution)/shard_map/ppermute | solution.py:359
  672.0 343.2 %collective-permute-start.2 = (bf16[3072,768]{1,0:T(8,128)(2,1)}, bf16[3072,768]{1,0:T(8,128)(2,1)}, u32[]{:S(2)}, u32[]{:S(2)}) collective-permute-start(bf16[3072,768]{1,0:T(8,128)(2,1)} %get-tuple-element.44), channel_id=1, source_target_pairs={{0,8},{8,0},{1,9},{9,1},{2,10},{10,2},{3,11},{11,3},{4,12},{12,4},... | collective-permute-start | bytes 14155784 | tf_op jit(solution)/shard_map/ppermute | solution.py:360
  878.1 240.0 %collective-permute-start.4 = (f32[2,7680]{1,0:T(2,128)S(1)}, f32[2,7680]{1,0:T(2,128)S(1)}, u32[]{:S(2)}, u32[]{:S(2)}) collective-permute-start(f32[2,7680]{1,0:T(2,128)S(1)} %pad_maximum_fusion), channel_id=1, source_target_pairs={{0,8},{8,0},{1,9},{9,1},{2,10},{10,2},{3,11},{11,3},{4,12},{12,4},... | collective-permute-start | bytes 184328 | tf_op jit(solution)/shard_map/ppermute | solution.py:380
  879.5 349.6 %collective-permute-start.1 = (bf16[768,3072]{1,0:T(8,128)(2,1)}, bf16[768,3072]{1,0:T(8,128)(2,1)}, u32[]{:S(2)}, u32[]{:S(2)}) collective-permute-start(bf16[768,3072]{1,0:T(8,128)(2,1)} %get-tuple-element.42), channel_id=1, source_target_pairs={{0,8},{8,0},{1,9},{9,1},{2,10},{10,2},{3,11},{11,3},{4,12},{12,4},... | collective-permute-start | bytes 14155784 | tf_op jit(solution)/shard_map/ppermute | solution.py:359
  880.2 353.8 %collective-permute-start.3 = (bf16[3072,768]{1,0:T(8,128)(2,1)}, bf16[3072,768]{1,0:T(8,128)(2,1)}, u32[]{:S(2)}, u32[]{:S(2)}) collective-permute-start(bf16[3072,768]{1,0:T(8,128)(2,1)} %get-tuple-element.45), channel_id=1, source_target_pairs={{0,8},{8,0},{1,9},{9,1},{2,10},{10,2},{3,11},{11,3},{4,12},{12,4},... | collective-permute-start | bytes 14155784 | tf_op jit(solution)/shard_map/ppermute | solution.py:360
  940.6 59.6 %copy-start.21 = (f32[8,1,320]{2,0,1:T(8,128)S(1)}, f32[8,1,320]{2,0,1:T(8,128)}, u32[]{:S(2)}) copy-start(f32[8,1,320]{2,0,1:T(8,128)} %stack_reshape.12) | copy-start | bytes 30724
  1000.9 9.1 all-to-all-start.5
  1010.0 93.6 %all-to-all-start.6 = ((bf16[8,2,320,768]{3,2,1,0:T(8,128)(2,1)}), bf16[8,2,320,768]{3,2,1,0:T(8,128)(2,1)}, u32[]{:S(2)}, u32[]{:S(2)}) async-start(bf16[8,2,320,768]{3,2,1,0:T(8,128)(2,1)} %get-tuple-element.61), calls=%async_computation.6 | async-start | bytes 15728640 | tf_op jit(solution)/shard_map/all_to_all | solution.py:370
  1103.6 176.5 %all-to-all-start.7 = ((bf16[8,2,320,768]{3,2,1,0:T(8,128)(2,1)}), bf16[8,2,320,768]{3,2,1,0:T(8,128)(2,1)}, u32[]{:S(2)}, u32[]{:S(2)}) async-start(bf16[8,2,320,768]{3,2,1,0:T(8,128)(2,1)} %get-tuple-element.62), calls=%async_computation.7 | async-start | bytes 15728640 | tf_op jit(solution)/shard_map/all_to_all | solution.py:371
  1108.5 113.9 %all-reduce.2.cloned.1.call-start = ((), (), s32[]{:S(2)}) async-start(), calls=%async_computation.8 | async-start | bytes 196608 | tf_op jit(solution)/shard_map/psum | solution.py:401
  1110.7 112.7 %copy-start.30 = (f32[768]{0:T(1024)S(1)}, f32[768]{0:T(1024)}, u32[]{:S(2)}) copy-start(f32[768]{0:T(1024)} %param.26) | copy-start | bytes 9220
  1110.7 114.0 %copy-start.34 = (f32[32]{0:T(128)S(1)}, f32[32]{0:T(128)}, u32[]{:S(2)}) copy-start(f32[32]{0:T(128)} %param.27) | copy-start | bytes 388
  1110.7 116.8 %copy-start.3 = (f32[768,32]{0,1:T(8,128)S(1)}, f32[768,32]{0,1:T(8,128)}, u32[]{:S(2)}) copy-start(f32[768,32]{0,1:T(8,128)} %param.19) | copy-start | bytes 294916
  (25 other events, 318.6 us)
Sparse Core Ops, SparseCore 0:
  1118.3 104.0 all-reduce.1

commit v4 on v3

--- a/solution.py
+++ b/solution.py
@@ -15,8 +15,8 @@
 AUX_COEF = 0.01
 F32 = jnp.float32
 BF16 = jnp.bfloat16
-OPT_TILE = (640, 1024, 3)
-ROWS_TILE = (640, 1536, 2)
+ROW_BLOCK = 640
+FORMS = ((208, 1024, 3), (256, 512, 1), (320, 512, 1))
 G_CHUNK = 64
 
 
@@ -60,8 +60,7 @@
         (x_ref, y_ref, p_ref, w_in, w_out, dbuf, g_out, w1, w2, sems, h_acc, b_acc) = refs
     step = pl.program_id(0)
     width, ff = w1.shape
-    f_chunk = OPT_TILE[1] if opt else ROWS_TILE[1]
-    chunks = ff // f_chunk
+
 
     @pl.when(step == 0)
     def _():
@@ -75,19 +74,20 @@
             acc_in[...] = jnp.zeros_like(acc_in)
             acc_out[...] = jnp.zeros_like(acc_out)
 
-    def body(own):
-        rows = p_ref.shape[0]
-        p = p_ref[...]
-        x = jnp.where(p > 0, x_ref[...].reshape(rows, width).astype(F32), 0.0).astype(BF16)
-        dh = (p * y_ref[...].reshape(rows, width).astype(F32)).astype(BF16)
+    def body(own, live, f_chunk, unroll):
+        per, _, cap, _ = x_ref.shape
+        rows = per * live
+        p = p_ref[...].reshape(per, cap, 1)[:, :live].reshape(rows, 1)
+        x = jnp.where(p > 0, x_ref[:, 0, :live, :].reshape(rows, width).astype(F32), 0.0).astype(BF16)
+        dh = (p * y_ref[:, 0, :live, :].reshape(rows, width).astype(F32)).astype(BF16)
         if opt:
             x_t = x.T
             dh_t = dh.T
         if own:
-            h_acc[...] = jnp.zeros_like(h_acc)
-            b_acc[...] = jnp.zeros_like(b_acc)
-
-        @pl.loop(0, chunks, unroll=OPT_TILE[2] if opt else ROWS_TILE[2])
+            h_acc[:rows] = jnp.zeros((rows, width), F32)
+            b_acc[:rows] = jnp.zeros((rows, width), F32)
+
+        @pl.loop(0, ff // f_chunk, unroll=unroll)
         def _(c):
             at = pl.ds(pl.multiple_of(c * f_chunk, f_chunk), f_chunk)
             w1c = w1[:, at]
@@ -96,26 +96,43 @@
             ga = kdot(dh, w2c, 1, 1)
             da = jnp.where(act.astype(F32) > 0, ga, 0.0).astype(BF16)
             if own:
-                h_acc[...] += kdot(act, w2c, 1, 0)
-                b_acc[...] += kdot(da, w1c, 1, 1)
+                h_acc[:rows] += kdot(act, w2c, 1, 0)
+                b_acc[:rows] += kdot(da, w1c, 1, 1)
             if opt:
                 acc_in[:, at] += kdot(x_t, da, 1, 0)
                 acc_out[:, at] += kdot(dh_t, act, 1, 0)
 
         if own:
-            h = h_acc[...].astype(BF16).astype(F32)
-            y = y_ref[...].reshape(rows, width).astype(F32)
-            g_out[...] = jnp.sum(y * h, axis=1, keepdims=True)
-            dbuf[...] = b_acc[...].astype(BF16).reshape(dbuf.shape)
+            h = h_acc[:rows].astype(BF16).astype(F32)
+            y = y_ref[:, 0, :live, :].reshape(rows, width).astype(F32)
+            g = jnp.sum(y * h, axis=1, keepdims=True).reshape(per, live, 1)
+            db = b_acc[:rows].astype(BF16).reshape(per, live, width)
+            for i in range(per):
+                g_out[i * cap:i * cap + live] = g[i]
+                dbuf[i, 0, :live, :] = db[i]
+                if live < cap:
+                    g_out[i * cap + live:(i + 1) * cap] = jnp.zeros((cap - live, 1), F32)
+                    dbuf[i, 0, live:, :] = jnp.zeros((cap - live, width), BF16)
+
+    def forms(own):
+        low = -1
+        for live, f_chunk, unroll in FORMS:
+            used = ids[2 + step]
+
+            @pl.when((used > low) & (used <= live))
+            def _(live=live, f_chunk=f_chunk, unroll=unroll):
+                body(own, live, f_chunk, unroll)
+
+            low = live
 
     if opt:
         @pl.when(step < own_blocks)
         def _():
-            body(True)
+            forms(True)
 
         @pl.when(step >= own_blocks)
         def _():
-            body(False)
+            forms(False)
 
         @pl.when(step == pl.num_programs(0) - 1)
         def _():
@@ -174,14 +191,14 @@
             o3.wait()
             o4.wait()
     else:
-        body(True)
+        forms(True)
 
 
 def expert_call(ids, x, y, p, w_in, w_out, column, back=None, stats=None, full=None):
     opt = stats is not None
     groups, _, cap, _ = x[0].shape
     el, width, ff = w_in.shape
-    row_block = OPT_TILE[0] if opt else ROWS_TILE[0]
+    row_block = ROW_BLOCK
     per = row_block // cap
     steps = groups // per
     nb = steps // 2 if opt else steps
@@ -190,6 +207,10 @@
         at = lambda i, ids: jnp.where(i < nb, ids[1] * nb + i, (1 - ids[1]) * nb + i - nb)
     else:
         at = lambda i, ids: i
+    used = jnp.max(jnp.where(p.reshape(steps, per, cap) > 0, jnp.arange(1, cap + 1, dtype=jnp.int32), 0), axis=(1, 2))
+    if opt:
+        used = jnp.roll(used, -nb * ids[1])
+    ids = jnp.concatenate([ids, used])
     in_specs = [pl.BlockSpec((per, 1, cap, width), lambda i, ids, c=c, w=w: (at(i, ids), c, 0, w)) for _, c, w in (x, y)]
     in_specs.append(pl.BlockSpec((row_block, 1), lambda i, ids: (at(i, ids), 0)))
     args = [x[0], y[0], p]
@@ -307,12 +328,12 @@
         is_c = token_slot[:, None] == jnp.arange(cap)[None, :]
         tok_idx = jnp.arange(tokens, dtype=jnp.int32)
 
-        def to_slots(vals):
+        def to_slots(vals, is_c):
             cols = jnp.concatenate([jnp.where(is_c, v.astype(BF16)[:, None], jnp.zeros((), BF16)) for v in vals], axis=1)
             out = mm(onehot_b, cols, ((0,), (0,)))
             return [out[:, i * cap:(i + 1) * cap] for i in range(len(vals))]
 
-        t_hi, t_lo = to_slots([tok_idx // 64, tok_idx % 64])
+        t_hi, t_lo = to_slots([tok_idx // 64, tok_idx % 64], is_c)
         src = (t_hi * 64.0 + t_lo).astype(jnp.int32).reshape(ep_size, dp_size, own, cap)
 
         def rows_of(table, index):
@@ -326,7 +347,7 @@
             buf = buf.reshape(dp_size * ep_size, 1, cap, -1)
             return lax.all_to_all(buf, ('dp', 'ep'), 0, 0, tiled=True), buf
 
-        x_first, _ = to_owners(x_tokens, 0)
+        x_first, x_buf = to_owners(x_tokens, 0)
         y_first, y_buf = to_owners(grad_y, 0)
         xy_tok = pair_rows(x_tokens, grad_y, y_buf)
         xy_own = [None] + [to_owners(xy_tok, k)[0] for k in range(1, own)]
@@ -338,12 +359,19 @@
         logits = lg[:, :experts] + (lg[:, experts:2 * experts] + lg[:, 2 * experts:])
         gate_probs = jax.nn.softmax(logits, axis=-1)
         gate_val = jnp.sum(gate_probs * onehot, axis=-1)
-        p_hi, p_mid, p_lo = to_slots(list(split3(gate_val)))
+        slot_later, _ = lax.optimization_barrier((token_slot, x_buf))
+        p_hi, p_mid, p_lo = to_slots(list(split3(gate_val)), slot_later[:, None] == jnp.arange(cap)[None, :])
         p_slot = (p_hi + (p_mid + p_lo)).reshape(ep_size, dp_size, own, cap)
         p_all = jnp.broadcast_to(p_slot[None], (dp_size,) + p_slot.shape).reshape(dp_size * ep_size, dp_size, own, cap)
         p_all = lax.all_to_all(p_all, ('dp', 'ep'), 0, 0, tiled=True)
         p_own = lax.dynamic_index_in_dim(p_all, zi, 1, keepdims=False)
         p_non = lax.dynamic_slice_in_dim(lax.dynamic_index_in_dim(p_all, 1 - zi, 1, keepdims=False), zi * ep_size, ep_size, 0)
+
+        p_rows = []
+        for k in range(own):
+            p_rows.append(p_own[:, k].reshape(-1, 1))
+        for k in range(own):
+            p_rows.append(p_non[:, k].reshape(-1, 1))
 
         def stat(table, e):
             return lax.dynamic_index_in_dim(table, e, 0)
@@ -354,7 +382,7 @@
             e = base + k
             ids = jnp.stack([e, zi])
             st = (stat(row_in, e).reshape(width, 1), stat(col_in, e), stat(col_out, e).reshape(width, 1), stat(row_out, e))
-            back_b, g, ni, no, fi, fo, s_in, l_in, s_out, l_out = expert_call(ids, *(((xy_own[k], 0, 0), (xy_own[k], 0, 1)) if k else ((x_first, 0, 0), (y_first, 0, 0))), p_own[:, k].reshape(-1, 1), w_in, w_out, k, back=back_b, stats=st, full=full)
+            back_b, g, ni, no, fi, fo, s_in, l_in, s_out, l_out = expert_call(ids, *(((xy_own[k], 0, 0), (xy_own[k], 0, 1)) if k else ((x_first, 0, 0), (y_first, 0, 0))), p_rows[k], w_in, w_out, k, back=back_b, stats=st, full=full)
             full = (fi, fo)
             new_in.append(lax.ppermute(ni, 'dp', swap))
             new_out.append(lax.ppermute(no, 'dp', swap))
@@ -364,7 +392,7 @@
         for k in range(own):
             e = lax.rem(base + own + k, el)
             ids, _ = lax.optimization_barrier((jnp.stack([e, zi]), last))
-            back_a, g = expert_call(ids, (xy_non, k, 0), (xy_non, k, 1), p_non[:, k].reshape(-1, 1), w_in, w_out, k, back=back_a)
+            back_a, g = expert_call(ids, (xy_non, k, 0), (xy_non, k, 1), p_rows[own + k], w_in, w_out, k, back=back_a)
             last = g
             g_pos.append(g)
         back_b = lax.all_to_all(back_b, 'ep', 0, 0, tiled=True)

time: 1350 us -> 1330 us (0.985)
  Pallas kernels: 530 us -> 435 us
  blocking collectives: 0 us -> 93.1 us
  waiting for transfers between devices: 395 us -> 359 us
    pallas_call x4, Pallas kernels: 508 us -> 413 us  [expert_call(): pl.pallas_call(functools.partial(expert_kernel, opt, back is not None, nb...]
    all_to_all x0 -> x1, blocking collectives: none -> 93.1 us  [to_owners(): return (lax.all_to_all(buf, ('dp', 'ep'), 0, 0, tiled=True), buf)]
    all_to_all x3 -> x2, waiting for transfers between devices: 216 us -> 147 us  [to_owners(): return (lax.all_to_all(buf, ('dp', 'ep'), 0, 0, tiled=True), buf)]
    psum x1, waiting for transfers between devices: 102 us -> 135 us  [step_body(): lax.psum(gr[:, :experts] + (gr[:, experts:2 * experts] + gr[:, 2 * expert...]
  transfers between devices with their start and end apart: 14 -> 13, of which waited for: 6 -> 5; matrix products, arithmetic and copies ran while one was open for 20% -> 18% of each run, Pallas kernels for 39% -> 33%
where the time goes in v4:
time: 1330 us; the launch traced here: 1320 us
  Pallas kernels  435 us (33%)
  waiting for transfers between devices  359 us (27%)
  local copies, waits for them, and re-layouts  275 us (21%)
  blocking collectives  93.1 us (7%)
  starting transfers between devices  56.7 us (4%)
  other arithmetic  44.8 us (3%)
  matrix products  43.7 us (3%)
  between operations  17.1 us (1%)
    pallas_call x4, Pallas kernels, expert_call(): pl.pallas_call(functools.partial(expert_kernel, opt, back is not None, nb...  413 us
    all_to_all x2, waiting for transfers between devices, to_owners(): return (lax.all_to_all(buf, ('dp', 'ep'), 0, 0, tiled=True), buf)  147 us
    gather x4, local copies, waits for them, and re-layouts, rows_of(): jnp.take(table, index.reshape(-1), axis=0, mode='clip')  145 us
    psum x1, waiting for transfers between devices, step_body(): lax.psum(gr[:, :experts] + (gr[:, experts:2 * experts] + gr[:, 2 * expert...  135 us
    all_to_all x1, blocking collectives, to_owners(): return (lax.all_to_all(buf, ('dp', 'ep'), 0, 0, tiled=True), buf)  93.1 us
    gather x2, local copies, waits for them, and re-layouts, rows_back(): jnp.take(table.reshape(nowhere, width), index, axis=0, mode='fill', fill_...  83 us
    all_to_all x1, waiting for transfers between devices, step_body(): back_b = lax.all_to_all(back_b, 'ep', 0, 0, tiled=True)  76.7 us
    dot_general x6, matrix products, mm(): return lax.dot_general(a, b, (dims, ((), ())), preferred_element_type=F32)  43.7 us
  transfers between devices with their start and end apart: 13, of which 5 were waited for; matrix products, arithmetic and copies ran while one was open for 18% of the time, Pallas kernels for 33%

profile of v4, /device:TPU:0, one launch (start us, length us, event | category | flops | bytes accessed | tf_op | source)
XLA Modules:
  0.0 1324.3 jit_solution(9001269767892690669)
XLA Ops:
  10.0 8.6 convolution_bitcast_fusion
  26.4 30.0 %gather_fusion = bf16[5120,768]{1,0:T(8,128)(2,1)} fusion(bf16[8192,768]{1,0:T(8,128)(2,1)} %x.1, s32[5120]{0:T(1024)S(1)} %broadcast_clamp_fusion.4), kind=kCustom, calls=%fused_computation.2 | custom fusion | bytes 15749120 | tf_op jit(solution)/shard_map/jit(_take)/gather | solution.py:340
  56.5 5.4 fusion.12
  61.9 8.0 fusion
  75.9 29.7 %gather_fusion.1 = bf16[5120,768]{1,0:T(8,128)(2,1)} fusion(bf16[8192,768]{1,0:T(8,128)(2,1)} %y.1, s32[5120]{0:T(1024)S(1)} %broadcast_clamp_fusion.4), kind=kCustom, calls=%fused_computation.3 | custom fusion | bytes 15749120 | tf_op jit(solution)/shard_map/jit(_take)/gather | solution.py:340
  105.7 93.1 %all_to_all.40.refs_1_ = bf16[16,1,320,768]{3,2,1,0:T(8,128)(2,1)} all-to-all(bf16[16,1,320,768]{3,2,1,0:T(8,128)(2,1)} %bitcast.64), channel_id=1, replica_groups=mesh['dp'=2,'ep'=8] {'dp','ep'}, dimensions={0} | all-to-all | bytes 15728640 | tf_op jit(solution)/shard_map/all_to_all | solution.py:348
  202.4 22.0 %pair_rows.1 = bf16[8192,1536]{1,0:T(8,128)(2,1)} custom-call(bf16[8192,768]{1,0:T(8,128)(2,1)} %x.1, bf16[8192,768]{1,0:T(8,128)(2,1)} %y.1, bf16[16,1,320,768]{3,2,1,0:T(8,128)(2,1)} %bitcast.65), custom_call_target="tpu_custom_call" | custom-call | flops 6291456 | bytes 50331648 | tf_op jit(solution)/shard_map/pair_rows/pallas_call | solution.py:270
  224.4 42.6 %gather_fusion.2 = bf16[5120,1536]{1,0:T(8,128)(2,1)} fusion(bf16[8192,1536]{1,0:T(8,128)(2,1)} %pair_rows.1, s32[5120]{0:T(1024)S(1)} %broadcast_clamp_fusion.3), kind=kCustom, calls=%fused_computation.4 | custom fusion | bytes 31477760 | tf_op jit(solution)/shard_map/jit(_take)/gather | solution.py:340
  267.1 30.4 %all-to-all-done.2.refs_0_ = bf16[16,1,320,768]{3,2,1,0:T(8,128)(2,1)} async-done(((bf16[16,1,320,768]{3,2,1,0:T(8,128)(2,1)}), bf16[16,1,320,768]{3,2,1,0:T(8,128)(2,1)}, u32[]{:S(2)}, u32[]{:S(2)}) %all-to-all-start.2) | async-done | bytes 7864352 | tf_op jit(solution)/shard_map/all_to_all | solution.py:348
  308.0 42.8 %gather_fusion.3 = bf16[5120,1536]{1,0:T(8,128)(2,1)} fusion(bf16[8192,1536]{1,0:T(8,128)(2,1)} %pair_rows.1, s32[5120]{0:T(1024)S(1)} %broadcast_clamp_fusion.2), kind=kCustom, calls=%fused_computation.5 | custom fusion | bytes 31477760 | tf_op jit(solution)/shard_map/jit(_take)/gather | solution.py:340
  373.5 117.1 %all-to-all-done.1.refs_0_.refs_1_ = bf16[16,1,320,1536]{3,2,1,0:T(8,128)(2,1)} async-done(((bf16[16,1,320,1536]{3,2,1,0:T(8,128)(2,1)}), bf16[16,1,320,1536]{3,2,1,0:T(8,128)(2,1)}, u32[]{:S(2)}, u32[]{:S(2)}) %all-to-all-start.1) | async-done | bytes 15728672 | tf_op jit(solution)/shard_map/all_to_all | solution.py:348
  490.5 5.7 all-to-all-start.4
  496.8 159.8 %expert_opt.2 = (bf16[8,2,320,768]{3,2,1,0:T(8,128)(2,1)}, f32[2560,1]{1,0:T(8,128)}, bf16[768,3072]{1,0:T(8,128)(2,1)}, bf16[3072,768]{1,0:T(8,128)(2,1)}, bf16...) custom-call(s32[10]{0:T(128)} %pad_add_fusion.3.ids, ...), custom_call_target="tpu_custom_call" | custom-call | flops 120795955200 | bytes 25165824 | tf_op jit(solution)/shard_map/expert_opt/pallas_call | solution.py:249
  664.1 166.1 %expert_opt.3 = (bf16[8,2,320,768]{3,2,1,0:T(8,128)(2,1)}, f32[2560,1]{1,0:T(8,128)}, bf16[768,3072]{1,0:T(8,128)(2,1)}, bf16[3072,768]{1,0:T(8,128)(2,1)}, bf16...) custom-call(s32[10]{0:T(128)} %pad_add_fusion.1.ids, ...), custom_call_target="tpu_custom_call", output_to_operand_aliasing={{0}: (6, {}), {4}: (11, {}), {5}: (12, {})} | custom-call | flops 120795955200 | bytes 25165824 | tf_op jit(solution)/shard_map/expert_opt/pallas_call | solution.py:249
  835.2 7.2 collective-permute-start.4
  845.1 40.2 %expert_rows.2 = (bf16[8,2,320,768]{3,2,1,0:T(8,128)(2,1)}, f32[2560,1]{1,0:T(8,128)}) custom-call(s32[6]{0:T(128)} %pad_add_fusion.5.ids, bf16[8,2,320,1536]{3,2,1,0:T(8,128)(2,1)} %all-to-all-done.4.refs_0_.refs_1_, bf16[8,2,320,1536]{3,2,1,0:T(8,128)(2,1)} %all-to-all-done.4.refs_0_.refs_1_, f32[2560,1]{1,0:T(8,128)} %reshape_squeeze.18.refs_2_, ...), custom_call_target="tpu_custom_call" | custom-call | flops 48318382080 | bytes 25165824 | tf_op jit(solution)/shard_map/expert_rows/pallas_call | solution.py:249
  887.7 47.0 %expert_rows.3 = (bf16[8,2,320,768]{3,2,1,0:T(8,128)(2,1)}, f32[2560,1]{1,0:T(8,128)}) custom-call(s32[6]{0:T(128)} %pad_add_fusion.7.ids, bf16[8,2,320,1536]{3,2,1,0:T(8,128)(2,1)} %all-to-all-done.4.refs_0_.refs_1_, bf16[8,2,320,1536]{3,2,1,0:T(8,128)(2,1)} %all-to-all-done.4.refs_0_.refs_1_, ...), custom_call_target="tpu_custom_call", output_to_operand_aliasing={{0}: (6, {})} | custom-call | flops 48318382080 | bytes 25165824 | tf_op jit(solution)/shard_map/expert_rows/pallas_call | solution.py:249
  937.2 16.1 %all-to-all-start.5 = ((f32[8,4,320]{2,1,0:T(4,128)}), f32[8,4,320]{2,1,0:T(4,128)S(1)}, u32[]{:S(2)}, u32[]{:S(2)}) async-start(f32[8,4,320]{2,1,0:T(4,128)} %copy.63), calls=%async_computation.5 | async-start | bytes 98304 | tf_op jit(solution)/shard_map/all_to_all | solution.py:417
  974.9 76.7 %all-to-all-done.6 = bf16[8,2,320,768]{3,2,1,0:T(8,128)(2,1)} async-done(((bf16[8,2,320,768]{3,2,1,0:T(8,128)(2,1)}), bf16[8,2,320,768]{3,2,1,0:T(8,128)(2,1)}, u32[]{:S(2)}, u32[]{:S(2)}) %all-to-all-start.6) | async-done | bytes 7864352 | tf_op jit(solution)/shard_map/all_to_all | solution.py:398
  1058.7 6.7 fusion.29
  1067.9 134.8 %all-reduce.2.cloned.1.call-done = f32[768,32]{0,1:T(8,128)} async-done(((f32[768,32]{0,1:T(8,128)}), f32[768,32]{0,1:T(8,128)}) %all-reduce.2.cloned.1.call-update) | async-done | bytes 98320 | tf_op jit(solution)/shard_map/psum | solution.py:429
  1219.1 41.6 %gather_fusion.4 = bf16[8192,768]{1,0:T(8,128)(2,1)} fusion(bf16[5120,768]{1,0:T(8,128)(2,1)} %bitcast.30, s32[8192]{0:T(1024)S(1)} %copy-done.18), kind=kCustom, calls=%fused_computation.clone | custom fusion | bytes 25198592 | tf_op jit(solution)/shard_map/jit(_take)/gather | solution.py:440
  1260.8 41.3 %gather_fusion.5 = bf16[8192,768]{1,0:T(8,128)(2,1)} fusion(bf16[5120,768]{1,0:T(8,128)(2,1)} %bitcast.31, s32[8192]{0:T(1024)S(1)} %copy-done.17), kind=kCustom, calls=%fused_computation.1.clone | custom fusion | bytes 25198592 | tf_op jit(solution)/shard_map/jit(_take)/gather | solution.py:440
  1302.1 15.2 %add_convert_fusion = bf16[8192,768]{1,0:T(8,128)(2,1)} fusion(bf16[8192,192]{0,1:T(8,128)(2,1)} %get-tuple-element.84, bf16[768,192]{0,1:T(8,128)(2,1)S(1)} %copy-done.26, bf16[8192,768]{1,0:T(8,128)(2,1)} %gather_fusion.5, bf16[8192,768]{1,0:T(8,128)(2,1)} %gather_fusion.4, pred[8192]{0:T(1024)(128)(4,1)S(1)} %copy-done.24, pred[8192]{0:T(1024)(128)(4,1)S(1)} %copy-done.27), kind=kOutput, calls=%fused_computation.6 | convolution fusion | flops 2453667840 | bytes 41205760 | tf_op jit(solution)/shard_map/dot_general | solution.py:304
  (210 shorter events, 119.1 us)
Async XLA Ops:
  70.7 35.0 %all-to-all-start = ((f32[16,2,2,320]{3,2,1,0:T(2,128)}), f32[16,2,2,320]{3,2,1,0:T(2,128)S(1)}, u32[]{:S(2)}, u32[]{:S(2)}) async-start(f32[16,2,2,320]{3,2,1,0:T(2,128)} %bitcast.6), calls=%async_computation | async-start | bytes 196608 | tf_op jit(solution)/shard_map/all_to_all | solution.py:366
  198.8 98.7 %all-to-all-start.2 = ((bf16[16,1,320,768]{3,2,1,0:T(8,128)(2,1)}), bf16[16,1,320,768]{3,2,1,0:T(8,128)(2,1)}, u32[]{:S(2)}, u32[]{:S(2)}) async-start(bf16[16,1,320,768]{3,2,1,0:T(8,128)(2,1)} %bitcast.68), calls=%async_computation.2 | async-start | bytes 15728640 | tf_op jit(solution)/shard_map/all_to_all | solution.py:348
  297.5 193.0 %all-to-all-start.1 = ((bf16[16,1,320,1536]{3,2,1,0:T(8,128)(2,1)}), bf16[16,1,320,1536]{3,2,1,0:T(8,128)(2,1)}, u32[]{:S(2)}, u32[]{:S(2)}) async-start(bf16[16,1,320,1536]{3,2,1,0:T(8,128)(2,1)} %bitcast.66), calls=%async_computation.1 | async-start | bytes 31457280 | tf_op jit(solution)/shard_map/all_to_all | solution.py:348
  307.9 44.1 %copy-start.13 = (bf16[768,32]{0,1:T(8,128)(2,1)S(1)}, bf16[768,32]{0,1:T(8,128)(2,1)}, u32[]{:S(2)}) copy-start(bf16[768,32]{0,1:T(8,128)(2,1)} %copy-done.12) | copy-start | bytes 147460
  307.9 44.7 %copy-start.11 = (bf16[768,32]{0,1:T(8,128)(2,1)S(1)}, bf16[768,32]{0,1:T(8,128)(2,1)}, u32[]{:S(2)}) copy-start(bf16[768,32]{0,1:T(8,128)(2,1)} %copy-done.10) | copy-start | bytes 147460
  307.9 45.3 %copy-start.31 = (f32[32]{0:T(128)S(1)}, f32[32]{0:T(128)}, u32[]{:S(2)}) copy-start(f32[32]{0:T(128)} %get-tuple-element.70) | copy-start | bytes 388
  308.0 47.8 %copy-start.21 = (f32[4,3072]{1,0:T(4,128)S(1)}, f32[4,3072]{1,0:T(4,128)}, u32[]{:S(2)}) copy-start(f32[4,3072]{1,0:T(4,128)} %param.26) | copy-start | bytes 147460
  308.0 47.8 %copy-start.22 = (f32[4,3072]{1,0:T(4,128)S(1)}, f32[4,3072]{1,0:T(4,128)}, u32[]{:S(2)}) copy-start(f32[4,3072]{1,0:T(4,128)} %param.25) | copy-start | bytes 147460
  490.5 354.5 %all-to-all-start.4 = ((bf16[8,2,320,1536]{3,2,1,0:T(8,128)(2,1)}), bf16[8,2,320,1536]{3,2,1,0:T(8,128)(2,1)}, u32[]{:S(2)}, u32[]{:S(2)}) async-start(bf16[8,2,320,1536]{3,2,1,0:T(8,128)(2,1)} %bitcast.67), calls=%async_computation.4 | async-start | bytes 31457280 | tf_op jit(solution)/shard_map/all_to_all | solution.py:355
  662.1 291.2 %collective-permute-start = (bf16[768,3072]{1,0:T(8,128)(2,1)}, bf16[768,3072]{1,0:T(8,128)(2,1)}, u32[]{:S(2)}, u32[]{:S(2)}) collective-permute-start(bf16[768,3072]{1,0:T(8,128)(2,1)} %get-tuple-element.44), channel_id=1, source_target_pairs={{0,8},{8,0},{1,9},{9,1},{2,10},{10,2},{3,11},{11,3},{4,12},{12,4},... | collective-permute-start | bytes 14155784 | tf_op jit(solution)/shard_map/ppermute | solution.py:387
  662.1 301.1 %collective-permute-start.2 = (bf16[3072,768]{1,0:T(8,128)(2,1)}, bf16[3072,768]{1,0:T(8,128)(2,1)}, u32[]{:S(2)}, u32[]{:S(2)}) collective-permute-start(bf16[3072,768]{1,0:T(8,128)(2,1)} %get-tuple-element.47), channel_id=1, source_target_pairs={{0,8},{8,0},{1,9},{9,1},{2,10},{10,2},{3,11},{11,3},{4,12},{12,4},... | collective-permute-start | bytes 14155784 | tf_op jit(solution)/shard_map/ppermute | solution.py:388
  664.1 180.4 %copy-start.34 = (s32[4]{0:T(128)S(1)}, s32[4]{0:T(128)}, u32[]{:S(2)}) copy-start(s32[4]{0:T(128)} %reduce_max.82) | copy-start | bytes 52
  664.1 180.4 %copy-start.36 = (s32[2]{0:T(128)S(1)}, s32[2]{0:T(128)}, u32[]{:S(2)}) copy-start(s32[2]{0:T(128)} %pad_add_fusion.4) | copy-start | bytes 28
  835.2 230.9 %collective-permute-start.4 = (f32[2,7680]{1,0:T(2,128)S(1)}, f32[2,7680]{1,0:T(2,128)S(1)}, u32[]{:S(2)}, u32[]{:S(2)}) collective-permute-start(f32[2,7680]{1,0:T(2,128)S(1)} %pad_maximum_fusion), channel_id=1, source_target_pairs={{0,8},{8,0},{1,9},{9,1},{2,10},{10,2},{3,11},{11,3},{4,12},{12,4},... | collective-permute-start | bytes 184328 | tf_op jit(solution)/shard_map/ppermute | solution.py:408
  842.5 366.9 %collective-permute-start.1 = (bf16[768,3072]{1,0:T(8,128)(2,1)}, bf16[768,3072]{1,0:T(8,128)(2,1)}, u32[]{:S(2)}, u32[]{:S(2)}) collective-permute-start(bf16[768,3072]{1,0:T(8,128)(2,1)} %get-tuple-element.45), channel_id=1, source_target_pairs={{0,8},{8,0},{1,9},{9,1},{2,10},{10,2},{3,11},{11,3},{4,12},{12,4},... | collective-permute-start | bytes 14155784 | tf_op jit(solution)/shard_map/ppermute | solution.py:387
  842.5 371.8 %collective-permute-start.3 = (bf16[3072,768]{1,0:T(8,128)(2,1)}, bf16[3072,768]{1,0:T(8,128)(2,1)}, u32[]{:S(2)}, u32[]{:S(2)}) collective-permute-start(bf16[3072,768]{1,0:T(8,128)(2,1)} %get-tuple-element.48), channel_id=1, source_target_pairs={{0,8},{8,0},{1,9},{9,1},{2,10},{10,2},{3,11},{11,3},{4,12},{12,4},... | collective-permute-start | bytes 14155784 | tf_op jit(solution)/shard_map/ppermute | solution.py:388
  887.7 48.9 %copy-start.19 = (f32[8,1,320]{2,0,1:T(8,128)S(1)}, f32[8,1,320]{2,0,1:T(8,128)}, u32[]{:S(2)}) copy-start(f32[8,1,320]{2,0,1:T(8,128)} %stack_reshape.12) | copy-start | bytes 30724
  937.2 21.0 %all-to-all-start.5 = ((f32[8,4,320]{2,1,0:T(4,128)}), f32[8,4,320]{2,1,0:T(4,128)S(1)}, u32[]{:S(2)}, u32[]{:S(2)}) async-start(f32[8,4,320]{2,1,0:T(4,128)} %copy.63), calls=%async_computation.5 | async-start | bytes 98304 | tf_op jit(solution)/shard_map/all_to_all | solution.py:417
  958.2 93.4 %all-to-all-start.6 = ((bf16[8,2,320,768]{3,2,1,0:T(8,128)(2,1)}), bf16[8,2,320,768]{3,2,1,0:T(8,128)(2,1)}, u32[]{:S(2)}, u32[]{:S(2)}) async-start(bf16[8,2,320,768]{3,2,1,0:T(8,128)(2,1)} %get-tuple-element.64), calls=%async_computation.6 | async-start | bytes 15728640 | tf_op jit(solution)/shard_map/all_to_all | solution.py:398
  1051.6 209.2 %all-to-all-start.7 = ((bf16[8,2,320,768]{3,2,1,0:T(8,128)(2,1)}), bf16[8,2,320,768]{3,2,1,0:T(8,128)(2,1)}, u32[]{:S(2)}, u32[]{:S(2)}) async-start(bf16[8,2,320,768]{3,2,1,0:T(8,128)(2,1)} %get-tuple-element.65), calls=%async_computation.7 | async-start | bytes 15728640 | tf_op jit(solution)/shard_map/all_to_all | solution.py:399
  1056.5 146.2 %all-reduce.2.cloned.1.call-start = ((), (), s32[]{:S(2)}) async-start(), calls=%async_computation.8 | async-start | bytes 196608 | tf_op jit(solution)/shard_map/psum | solution.py:429
  1058.7 145.0 %copy-start.28 = (f32[768]{0:T(1024)S(1)}, f32[768]{0:T(1024)}, u32[]{:S(2)}) copy-start(f32[768]{0:T(1024)} %param.28) | copy-start | bytes 9220
  1058.7 146.2 %copy-start.32 = (f32[32]{0:T(128)S(1)}, f32[32]{0:T(128)}, u32[]{:S(2)}) copy-start(f32[32]{0:T(128)} %param.29) | copy-start | bytes 388
  1058.7 149.1 %copy-start.3 = (f32[768,32]{0,1:T(8,128)S(1)}, f32[768,32]{0,1:T(8,128)}, u32[]{:S(2)}) copy-start(f32[768,32]{0,1:T(8,128)} %param.21) | copy-start | bytes 294916
  (26 other events, 366.1 us)
Sparse Core Ops, SparseCore 0:
  1066.3 136.3 all-reduce.1
